TPU v7x, 256 devices: a whole 4x4x8 slice. The times are simulated.
256 devices in a mesh: row: 16 (over y, x), col: 16 (over z, core).
Axes of the slice: x: 4, y: 4, z: 8, core: 2. Of those that a mesh axis runs over, the one named last changes fastest.
Arguments:
- tile_data: bfloat16 [1024, 128, 128], P(('row', 'col')), may hold values from -24 to 24
- tile_coords: int32 [3, 1024], P(None, ('row', 'col')), may hold values from 0 to 2047, as said below
- tile_counts: int32 [256], P(('row', 'col')), may hold values from 1 to 4, as said below
- factor_rows: float32 [64, 32768], P(None, ('row', 'col')), may hold values from -6 to 6
- factor_cols: float32 [64, 32768], P(None, ('col', 'row')), may hold values from -6 to 6
- factor_depth: float32 [64, 2048], P(None, ('row', 'col')), may hold values from -6 to 6
- damping: float32 [], replicated, may hold values from 128 to 512
Outputs:
- step_a: float32 [64, 32768], P(None, ('row', 'col'))
- step_b: float32 [64, 32768], P(None, ('col', 'row'))
- step_c: float32 [64, 2048], P(None, ('row', 'col'))
Inputs may be any that keep to these rules, and one draw needn't show every extreme that they name: `tile_coords`: the first row names a tile's block within its device's group of 16 first-mode blocks, the second its block within the group of 16 second-mode blocks, the third its third-mode index below 2048. `tile_counts`: slots at and beyond a device's count are padding and carry nothing; some device fills all 4 slots.
All inputs are finite; a program needn't handle non-finite values.
Results may differ from a plain program's by a relative error of at most 0.0003.
Values sent between devices are 32-bit elements; how exact they have to be, the bound alone decides.
A program may use at most 64 MiB of HBM per device.

v0:
```python
import jax
import jax.numpy as jnp
from jax import lax
from jax.sharding import Mesh
from jax.sharding import PartitionSpec as P

RB = 16
CB = 16
ITERS = 2
ROW_COL = ("row_0", "row_1", "col_0", "col_1")
COL = ("col_0", "col_1")
ROW = ("row_0", "row_1")
COL_ROW = ("col_0", "col_1", "row_0", "row_1")


exact_precision = lax.Precision.HIGHEST


def from_everyone(value, axis):
    count = lax.axis_size(axis)
    return lax.all_to_all(
        jnp.broadcast_to(value[None], (count, *value.shape)), axis, 0, 0, tiled=True
    )


def taken_together(value, axis):
    everything = from_everyone(value, axis)
    return jnp.sum(everything, axis=0)


def over_axes(value, axes):
    far, near = axes
    nearer = taken_together(value, near)
    return taken_together(nearer, far)


def joined_along(parts, dim):
    lengths = list(parts.shape[1:])
    lengths[dim] *= parts.shape[0]
    return jnp.moveaxis(parts, 0, dim).reshape(lengths)


def collect(value, axis, dim):
    return joined_along(from_everyone(value, axis), dim)


def whole_of(value, axes, dim):
    far, near = axes
    leading = from_everyone(value, far)
    parts = jnp.swapaxes(from_everyone(leading, near), 0, 1)
    return joined_along(parts.reshape(-1, *value.shape), dim)


def in_blocks(value, dim, count):
    before, after = (value.shape[:dim], value.shape[dim + 1 :])
    return jnp.moveaxis(value.reshape(*before, count, -1, *after), dim, 0)


def sent_and_summed(value, axis, dim):
    count = lax.axis_size(axis)
    parts = lax.all_to_all(in_blocks(value, dim, count), axis, 0, 0, tiled=True)
    return jnp.sum(parts, axis=0)


def make_onehot(indices, block_count):
    return (indices[:, None] == jnp.arange(block_count, dtype=jnp.int32)[None, :]).astype(
        jnp.float32
    )


def pick_rows(onehot, blocks):
    shaped = blocks.reshape(blocks.shape[0], onehot.shape[1], blocks.shape[1] // onehot.shape[1])
    return jnp.einsum("tq,rqa->tra", onehot, shaped, precision=exact_precision)


def fold_rows(onehot, grads):
    summed = jnp.einsum("tq,tra->rqa", onehot, grads, precision=exact_precision)
    return summed.reshape(summed.shape[0], summed.shape[1] * summed.shape[2])


def tile_model(rows_a, rows_b, rows_c):
    return jnp.einsum(
        "tra,trb->tab", rows_a, rows_b * rows_c[:, :, None], precision=exact_precision
    )


def tile_products(rows_a, rows_b, rows_c, dir_a, dir_b, dir_c):
    depth_cols = rows_c[:, :, None]
    left_side = jnp.concatenate([dir_a, rows_a, rows_a], axis=1)
    right_side = jnp.concatenate(
        [rows_b * depth_cols, dir_b * depth_cols, rows_b * dir_c[:, :, None]], axis=1
    )
    return jnp.einsum("tra,trb->tab", left_side, right_side, precision=exact_precision)


def tile_transpose(values, rows_a, rows_b, rows_c):
    depth_cols = rows_c[:, :, None]
    row_raw = jnp.einsum("tab,trb->tra", values, rows_b, precision=exact_precision)
    grad_rows = row_raw * depth_cols
    grad_cols = jnp.einsum("tab,tra->trb", values, rows_a * depth_cols, precision=exact_precision)
    grad_depth = jnp.sum(rows_a * row_raw, axis=2)
    return (grad_rows, grad_cols, grad_depth)


def local_inner(first, second):
    return (
        jnp.sum(first[0] * second[0])
        + jnp.sum(first[1] * second[1])
        + jnp.sum(first[2] * second[2])
    )


def squares(residual):
    return over_axes(local_inner(residual, residual), ("row_0", ("row_1", "col_0", "col_1")))


def per_device(
    tile_data, tile_coords, tile_counts, factor_rows, factor_cols, factor_depth, damping
):
    whole_a = collect(factor_rows, COL, 1)
    whole_b = collect(factor_cols, ROW, 1)
    whole_c = whole_of(factor_depth, ("row_0", ("row_1", "col_0", "col_1")), 1)
    piece_width = factor_depth.shape[1]
    own_start = lax.axis_index(ROW_COL) * piece_width
    live_mask = (jnp.arange(tile_data.shape[0], dtype=jnp.int32) < tile_counts[0]).astype(
        jnp.float32
    )[:, None, None]
    pick_a = make_onehot(tile_coords[0], RB)
    pick_b = make_onehot(tile_coords[1], CB)
    rows_a = pick_rows(pick_a, whole_a)
    rows_b = pick_rows(pick_b, whole_b)
    rows_c = jnp.take(whole_c, tile_coords[2], axis=1).T
    every_index = whole_of(tile_coords[2], ("row_0", ("row_1", "col_0", "col_1")), 0)

    def add_depth(piece):
        placed = (
            (every_index - own_start)[:, None] == jnp.arange(piece_width, dtype=jnp.int32)[None, :]
        ).astype(jnp.float32)
        return jnp.einsum("tr,tw->rw", piece, placed, precision=exact_precision)

    def send_back(values):
        grad_rows, grad_cols, grad_depth = tile_transpose(
            values * live_mask, rows_a, rows_b, rows_c
        )
        share_a = sent_and_summed(fold_rows(pick_a, grad_rows), COL, 1)
        share_b = sent_and_summed(fold_rows(pick_b, grad_cols), ROW, 1)
        share_c = add_depth(whole_of(grad_depth, ("row_0", ("row_1", "col_0", "col_1")), 0))
        return (share_a, share_b, share_c)

    rhs = send_back(tile_data.astype(jnp.float32) - tile_model(rows_a, rows_b, rows_c))
    solution = tuple((jnp.zeros_like(member) for member in rhs))
    residual = rhs
    direction = rhs
    norm_now = squares(residual)
    for iteration in range(ITERS):
        gathered_a = collect(direction[0], COL, 1)
        gathered_b = collect(direction[1], ROW, 1)
        gathered_c = whole_of(direction[2], ("row_0", ("row_1", "col_0", "col_1")), 1)
        hessian_values = tile_products(
            rows_a,
            rows_b,
            rows_c,
            pick_rows(pick_a, gathered_a),
            pick_rows(pick_b, gathered_b),
            jnp.take(gathered_c, tile_coords[2], axis=1).T,
        )
        applied = send_back(hessian_values)
        image_vec = tuple(
            (part_one + damping * part_two for part_one, part_two in zip(applied, direction))
        )
        curvature = over_axes(
            local_inner(direction, image_vec), ("row_0", ("row_1", "col_0", "col_1"))
        )
        step_size = norm_now / curvature
        solution = tuple((sol + step_size * dvec for sol, dvec in zip(solution, direction)))
        residual = tuple((res - step_size * ivec for res, ivec in zip(residual, image_vec)))
        norm_next = squares(residual)
        direction = tuple(
            (res + norm_next / norm_now * dvec for res, dvec in zip(residual, direction))
        )
        norm_now = norm_next
    return (solution[0], solution[1], solution[2])


def solution(mesh):
    finer = Mesh(mesh.devices.reshape(4, 4, 8, 2), ("row_0", "row_1", "col_0", "col_1"))
    in_specs = (
        P(ROW_COL, None, None),
        P(None, ROW_COL),
        P(ROW_COL),
        P(None, ROW_COL),
        P(None, COL_ROW),
        P(None, ROW_COL),
        P(),
    )
    out_specs = (P(None, ROW_COL), P(None, COL_ROW), P(None, ROW_COL))
    return jax.shard_map(
        per_device, mesh=finer, in_specs=in_specs, out_specs=out_specs, check_vma=False
    )
```

profile of v0, /device:TPU:1, one launch (start us, length us, event | category | flops | bytes accessed | tf_op | source)
XLA Modules:
  0.0 566.7 jit_solution(17091745319541720920)
XLA Ops:
  1.4 9.0 %all_to_all.179 = f32[4,1,512]{2,1,0:T(1,128)S(1)} all-to-all(f32[4,1,512]{2,1,0:T(1,128)S(1)} %reshape.155), channel_id=1, replica_groups=mesh['row_0'=4,'row_1'=4,'col_0'=8,'col_1'=2] {'row_0'}, dimensions={0} | all-to-all | bytes 16384 | tf_op jit(solution)/shard_map/all_to_all | solution.py:21
  10.4 14.4 %all_to_all.180 = f32[16,64,128]{2,1,0:T(8,128)S(1)} all-to-all(f32[16,64,128]{2,1,0:T(8,128)S(1)} %broadcast_in_dim.67), channel_id=1, replica_groups=mesh['row_0'=4,'row_1'=4,'col_0'=8,'col_1'=2] {'row_0','row_1'}, dimensions={0} | all-to-all | bytes 1048576 | tf_op jit(solution)/shard_map/all_to_all | solution.py:21
  25.7 11.4 %all-to-all-start.1 = ((f32[16,64,128]{2,1,0:T(8,128)}), f32[16,64,128]{2,1,0:T(8,128)S(1)}, u32[]{:S(2)}, u32[]{:S(2)}) async-start(f32[16,64,128]{2,1,0:T(8,128)} %broadcast_in_dim.68), calls=%async_computation.1 | async-start | bytes 1048576 | tf_op jit(solution)/shard_map/all_to_all | solution.py:21
  40.6 13.7 %all-to-all-done.1 = f32[16,64,128]{2,1,0:T(8,128)S(1)} async-done(((f32[16,64,128]{2,1,0:T(8,128)}), f32[16,64,128]{2,1,0:T(8,128)S(1)}, u32[]{:S(2)}, u32[]{:S(2)}) %all-to-all-start.1) | async-done | bytes 524320 | tf_op jit(solution)/shard_map/all_to_all | solution.py:21
  59.8 15.5 %all-to-all-done.3 = f32[64,1,2048]{2,1,0:T(1,128)S(1)} async-done(((f32[64,1,2048]{2,1,0:T(1,128)}), f32[64,1,2048]{2,1,0:T(1,128)S(1)}, u32[]{:S(2)}, u32[]{:S(2)}) %all-to-all-start.3) | async-done | bytes 524320 | tf_op jit(solution)/shard_map/all_to_all | solution.py:21
  83.3 16.2 %all_to_all.181 = f32[16,64,128]{2,1,0:T(8,128)S(1)} all-to-all(f32[16,64,128]{2,1,0:T(8,128)S(1)} %copy.296), channel_id=1, replica_groups=mesh['row_0'=4,'row_1'=4,'col_0'=8,'col_1'=2] {'row_0','row_1'}, dimensions={0} | all-to-all | bytes 1048576 | tf_op jit(solution)/shard_map/all_to_all | solution.py:61
  99.6 13.6 %all_to_all.182 = f32[16,64,128]{2,1,0:T(8,128)S(1)} all-to-all(f32[16,64,128]{2,1,0:T(8,128)S(1)} %broadcast_in_dim.79), channel_id=1, replica_groups=mesh['row_0'=4,'row_1'=4,'col_0'=8,'col_1'=2] {'row_0','row_1'}, dimensions={0} | all-to-all | bytes 1048576 | tf_op jit(solution)/shard_map/all_to_all | solution.py:21
  128.2 8.7 %all-to-all-start.9 = ((s32[64,4,4]{2,1,0:T(4,128)}), s32[64,4,4]{2,1,0:T(4,128)S(1)}, u32[]{:S(2)}, u32[]{:S(2)}) async-start(s32[64,4,4]{2,1,0:T(4,128)} %broadcast_in_dim.75), calls=%async_computation.9 | async-start | bytes 262144 | tf_op jit(solution)/shard_map/all_to_all | solution.py:21
  152.4 11.8 %all-to-all-done.7 = f32[64,1,1024]{2,1,0:T(1,128)S(1)} async-done(((f32[64,1,1024]{2,1,0:T(1,128)}), f32[64,1,1024]{2,1,0:T(1,128)S(1)}, u32[]{:S(2)}, u32[]{:S(2)}) %all-to-all-start.7) | async-done | bytes 262176 | tf_op jit(solution)/shard_map/all_to_all | solution.py:21
  182.8 14.9 %all-to-all-done.4 = f32[16,64,128]{2,1,0:T(8,128)S(1)} async-done(((f32[16,64,128]{2,1,0:T(8,128)}), f32[16,64,128]{2,1,0:T(8,128)S(1)}, u32[]{:S(2)}, u32[]{:S(2)}) %all-to-all-start.4) | async-done | bytes 524320 | tf_op jit(solution)/shard_map/all_to_all | solution.py:61
  202.7 17.2 %all-to-all-done.15 = f32[64,1,2048]{2,1,0:T(1,128)S(1)} async-done(((f32[64,1,2048]{2,1,0:T(1,128)}), f32[64,1,2048]{2,1,0:T(1,128)S(1)}, u32[]{:S(2)}, u32[]{:S(2)}) %all-to-all-start.15) | async-done | bytes 524320 | tf_op jit(solution)/shard_map/all_to_all | solution.py:21
  231.0 11.7 %all-to-all-done.12 = f32[16,64,128]{2,1,0:T(8,128)S(1)} async-done(((f32[16,64,128]{2,1,0:T(8,128)}), f32[16,64,128]{2,1,0:T(8,128)S(1)}, u32[]{:S(2)}, u32[]{:S(2)}) %all-to-all-start.12) | async-done | bytes 524320 | tf_op jit(solution)/shard_map/all_to_all | solution.py:21
  259.3 9.0 %all-to-all-done.17 = f32[16,64,128]{2,1,0:T(8,128)S(1)} async-done(((f32[16,64,128]{2,1,0:T(8,128)}), f32[16,64,128]{2,1,0:T(8,128)S(1)}, u32[]{:S(2)}, u32[]{:S(2)}) %all-to-all-start.17) | async-done | bytes 524320 | tf_op jit(solution)/shard_map/all_to_all | solution.py:61
  275.3 10.5 %all-to-all-done.19 = f32[64,1,1024]{2,1,0:T(1,128)S(1)} async-done(((f32[64,1,1024]{2,1,0:T(1,128)}), f32[64,1,1024]{2,1,0:T(1,128)S(1)}, u32[]{:S(2)}, u32[]{:S(2)}) %all-to-all-start.19) | async-done | bytes 262176 | tf_op jit(solution)/shard_map/all_to_all | solution.py:21
  295.0 12.7 %all-to-all-done.16 = f32[16,64,128]{2,1,0:T(8,128)S(1)} async-done(((f32[16,64,128]{2,1,0:T(8,128)}), f32[16,64,128]{2,1,0:T(8,128)S(1)}, u32[]{:S(2)}, u32[]{:S(2)}) %all-to-all-start.16) | async-done | bytes 524320 | tf_op jit(solution)/shard_map/all_to_all | solution.py:61
  310.8 16.4 %all-to-all-start.10 = ((f32[64,1,1]{2,1,0:T(1,128)}), f32[64,1,1]{2,1,0:T(1,128)S(1)}, u32[]{:S(2)}, u32[]{:S(2)}) async-start(f32[64,1,1]{2,1,0:T(1,128)} %broadcast_in_dim.76), calls=%async_computation.10 | async-start | bytes 65536 | tf_op jit(solution)/shard_map/all_to_all | solution.py:21
  342.5 8.6 %all-to-all-done.20 = f32[64,1,1]{2,1,0:T(1,128)S(1)} async-done(((f32[64,1,1]{2,1,0:T(1,128)}), f32[64,1,1]{2,1,0:T(1,128)S(1)}, u32[]{:S(2)}, u32[]{:S(2)}) %all-to-all-start.20) | async-done | bytes 288 | tf_op jit(solution)/shard_map/all_to_all | solution.py:21
  373.3 15.6 %all_to_all.184 = f32[64,1,1]{2,1,0:T(1,128)S(1)} all-to-all(f32[64,1,1]{2,1,0:T(1,128)S(1)} %broadcast_in_dim.86), channel_id=1, replica_groups=mesh['row_0'=4,'row_1'=4,'col_0'=8,'col_1'=2] {'row_1','col_0','col_1'}, dimensions={0} | all-to-all | bytes 512 | tf_op jit(solution)/shard_map/all_to_all | solution.py:21
  411.3 8.9 %all-to-all-done.25 = f32[16,64,128]{2,1,0:T(8,128)S(1)} async-done(((f32[16,64,128]{2,1,0:T(8,128)}), f32[16,64,128]{2,1,0:T(8,128)S(1)}, u32[]{:S(2)}, u32[]{:S(2)}) %all-to-all-start.25) | async-done | bytes 524320 | tf_op jit(solution)/shard_map/all_to_all | solution.py:21
  430.9 15.0 %all-to-all-done.24 = f32[16,64,128]{2,1,0:T(8,128)S(1)} async-done(((f32[16,64,128]{2,1,0:T(8,128)}), f32[16,64,128]{2,1,0:T(8,128)S(1)}, u32[]{:S(2)}, u32[]{:S(2)}) %all-to-all-start.24) | async-done | bytes 524320 | tf_op jit(solution)/shard_map/all_to_all | solution.py:21
  451.5 15.3 %all-to-all-done.27 = f32[64,1,2048]{2,1,0:T(1,128)S(1)} async-done(((f32[64,1,2048]{2,1,0:T(1,128)}), f32[64,1,2048]{2,1,0:T(1,128)S(1)}, u32[]{:S(2)}, u32[]{:S(2)}) %all-to-all-start.27) | async-done | bytes 524320 | tf_op jit(solution)/shard_map/all_to_all | solution.py:21
  505.7 10.5 %all-to-all-done.31 = f32[64,1,1024]{2,1,0:T(1,128)S(1)} async-done(((f32[64,1,1024]{2,1,0:T(1,128)}), f32[64,1,1024]{2,1,0:T(1,128)S(1)}, u32[]{:S(2)}, u32[]{:S(2)}) %all-to-all-start.31) | async-done | bytes 262176 | tf_op jit(solution)/shard_map/all_to_all | solution.py:21
  524.6 13.5 %all-to-all-done.28 = f32[16,64,128]{2,1,0:T(8,128)S(1)} async-done(((f32[16,64,128]{2,1,0:T(8,128)}), f32[16,64,128]{2,1,0:T(8,128)S(1)}, u32[]{:S(2)}, u32[]{:S(2)}) %all-to-all-start.28) | async-done | bytes 524320 | tf_op jit(solution)/shard_map/all_to_all | solution.py:61
  540.7 14.1 %all_to_all.186 = f32[64,1,1]{2,1,0:T(1,128)S(1)} all-to-all(f32[64,1,1]{2,1,0:T(1,128)S(1)} %broadcast_in_dim.94), channel_id=1, replica_groups=mesh['row_0'=4,'row_1'=4,'col_0'=8,'col_1'=2] {'row_1','col_0','col_1'}, dimensions={0} | all-to-all | bytes 512 | tf_op jit(solution)/shard_map/all_to_all | solution.py:21
  (206 shorter events, 243.7 us)
Async XLA Ops:
  25.7 28.6 %all-to-all-start.1 = ((f32[16,64,128]{2,1,0:T(8,128)}), f32[16,64,128]{2,1,0:T(8,128)S(1)}, u32[]{:S(2)}, u32[]{:S(2)}) async-start(f32[16,64,128]{2,1,0:T(8,128)} %broadcast_in_dim.68), calls=%async_computation.1 | async-start | bytes 1048576 | tf_op jit(solution)/shard_map/all_to_all | solution.py:21
  54.3 20.9 %all-to-all-start.3 = ((f32[64,1,2048]{2,1,0:T(1,128)}), f32[64,1,2048]{2,1,0:T(1,128)S(1)}, u32[]{:S(2)}, u32[]{:S(2)}) async-start(f32[64,1,2048]{2,1,0:T(1,128)} %reshape.157), calls=%async_computation.3 | async-start | bytes 1048576 | tf_op jit(solution)/shard_map/all_to_all | solution.py:21
  113.8 7.3 %all-to-all-start.8 = ((s32[4,1,4]{2,1,0:T(1,128)}), s32[4,1,4]{2,1,0:T(1,128)S(1)}, u32[]{:S(2)}, u32[]{:S(2)}) async-start(s32[4,1,4]{2,1,0:T(1,128)} %broadcast_in_dim.73), calls=%async_computation.8 | async-start | bytes 4096 | tf_op jit(solution)/shard_map/all_to_all | solution.py:21
  128.2 19.2 %all-to-all-start.9 = ((s32[64,4,4]{2,1,0:T(4,128)}), s32[64,4,4]{2,1,0:T(4,128)S(1)}, u32[]{:S(2)}, u32[]{:S(2)}) async-start(s32[64,4,4]{2,1,0:T(4,128)} %broadcast_in_dim.75), calls=%async_computation.9 | async-start | bytes 262144 | tf_op jit(solution)/shard_map/all_to_all | solution.py:21
  147.3 16.9 %all-to-all-start.7 = ((f32[64,1,1024]{2,1,0:T(1,128)}), f32[64,1,1024]{2,1,0:T(1,128)S(1)}, u32[]{:S(2)}, u32[]{:S(2)}) async-start(f32[64,1,1024]{2,1,0:T(1,128)} %reshape.161), calls=%async_computation.7 | async-start | bytes 524288 | tf_op jit(solution)/shard_map/all_to_all | solution.py:21
  167.3 7.4 %all-to-all-start.14 = ((f32[4,1,512]{2,1,0:T(1,128)}), f32[4,1,512]{2,1,0:T(1,128)S(1)}, u32[]{:S(2)}, u32[]{:S(2)}) async-start(f32[4,1,512]{2,1,0:T(1,128)} %reshape.163), calls=%async_computation.14 | async-start | bytes 16384 | tf_op jit(solution)/shard_map/all_to_all | solution.py:21
  174.7 22.9 %all-to-all-start.4 = ((f32[16,64,128]{2,1,0:T(8,128)}), f32[16,64,128]{2,1,0:T(8,128)S(1)}, u32[]{:S(2)}, u32[]{:S(2)}) async-start(f32[16,64,128]{2,1,0:T(8,128)} %copy.293), calls=%async_computation.4 | async-start | bytes 1048576 | tf_op jit(solution)/shard_map/all_to_all | solution.py:61
  197.6 22.3 %all-to-all-start.15 = ((f32[64,1,2048]{2,1,0:T(1,128)}), f32[64,1,2048]{2,1,0:T(1,128)S(1)}, u32[]{:S(2)}, u32[]{:S(2)}) async-start(f32[64,1,2048]{2,1,0:T(1,128)} %reshape.165), calls=%async_computation.15 | async-start | bytes 1048576 | tf_op jit(solution)/shard_map/all_to_all | solution.py:21
  220.8 21.9 %all-to-all-start.12 = ((f32[16,64,128]{2,1,0:T(8,128)}), f32[16,64,128]{2,1,0:T(8,128)S(1)}, u32[]{:S(2)}, u32[]{:S(2)}) async-start(f32[16,64,128]{2,1,0:T(8,128)} %broadcast_in_dim.78), calls=%async_computation.12 | async-start | bytes 1048576 | tf_op jit(solution)/shard_map/all_to_all | solution.py:21
  246.4 7.4 %all-to-all-start.18 = ((f32[4,1,256]{2,1,0:T(1,128)}), f32[4,1,256]{2,1,0:T(1,128)S(1)}, u32[]{:S(2)}, u32[]{:S(2)}) async-start(f32[4,1,256]{2,1,0:T(1,128)} %reshape.167), calls=%async_computation.18 | async-start | bytes 8192 | tf_op jit(solution)/shard_map/all_to_all | solution.py:21
  253.7 14.6 %all-to-all-start.17 = ((f32[16,64,128]{2,1,0:T(8,128)}), f32[16,64,128]{2,1,0:T(8,128)S(1)}, u32[]{:S(2)}, u32[]{:S(2)}) async-start(f32[16,64,128]{2,1,0:T(8,128)} %copy.314), calls=%async_computation.17 | async-start | bytes 1048576 | tf_op jit(solution)/shard_map/all_to_all | solution.py:61
  268.3 17.5 %all-to-all-start.19 = ((f32[64,1,1024]{2,1,0:T(1,128)}), f32[64,1,1024]{2,1,0:T(1,128)S(1)}, u32[]{:S(2)}, u32[]{:S(2)}) async-start(f32[64,1,1024]{2,1,0:T(1,128)} %reshape.169), calls=%async_computation.19 | async-start | bytes 524288 | tf_op jit(solution)/shard_map/all_to_all | solution.py:21
  285.8 21.8 %all-to-all-start.16 = ((f32[16,64,128]{2,1,0:T(8,128)}), f32[16,64,128]{2,1,0:T(8,128)S(1)}, u32[]{:S(2)}, u32[]{:S(2)}) async-start(f32[16,64,128]{2,1,0:T(8,128)} %copy.312), calls=%async_computation.16 | async-start | bytes 1048576 | tf_op jit(solution)/shard_map/all_to_all | solution.py:61
  310.8 25.7 %all-to-all-start.10 = ((f32[64,1,1]{2,1,0:T(1,128)}), f32[64,1,1]{2,1,0:T(1,128)S(1)}, u32[]{:S(2)}, u32[]{:S(2)}) async-start(f32[64,1,1]{2,1,0:T(1,128)} %broadcast_in_dim.76), calls=%async_computation.10 | async-start | bytes 65536 | tf_op jit(solution)/shard_map/all_to_all | solution.py:21
  337.1 14.1 %all-to-all-start.20 = ((f32[64,1,1]{2,1,0:T(1,128)}), f32[64,1,1]{2,1,0:T(1,128)S(1)}, u32[]{:S(2)}, u32[]{:S(2)}) async-start(f32[64,1,1]{2,1,0:T(1,128)} %broadcast_in_dim.84), calls=%async_computation.20 | async-start | bytes 65536 | tf_op jit(solution)/shard_map/all_to_all | solution.py:21
  352.4 7.3 %all-to-all-start.11 = ((f32[4,1,1]{2,1,0:T(1,128)}), f32[4,1,1]{2,1,0:T(1,128)S(1)}, u32[]{:S(2)}, u32[]{:S(2)}) async-start(f32[4,1,1]{2,1,0:T(1,128)} %broadcast_in_dim.77), calls=%async_computation.11 | async-start | bytes 4096 | tf_op jit(solution)/shard_map/all_to_all | solution.py:21
  399.5 7.4 %all-to-all-start.26 = ((f32[4,1,512]{2,1,0:T(1,128)}), f32[4,1,512]{2,1,0:T(1,128)S(1)}, u32[]{:S(2)}, u32[]{:S(2)}) async-start(f32[4,1,512]{2,1,0:T(1,128)} %reshape.171), calls=%async_computation.26 | async-start | bytes 16384 | tf_op jit(solution)/shard_map/all_to_all | solution.py:21
  407.7 12.5 %all-to-all-start.25 = ((f32[16,64,128]{2,1,0:T(8,128)}), f32[16,64,128]{2,1,0:T(8,128)S(1)}, u32[]{:S(2)}, u32[]{:S(2)}) async-start(f32[16,64,128]{2,1,0:T(8,128)} %broadcast_in_dim.89), calls=%async_computation.25 | async-start | bytes 1048576 | tf_op jit(solution)/shard_map/all_to_all | solution.py:21
  421.1 24.8 %all-to-all-start.24 = ((f32[16,64,128]{2,1,0:T(8,128)}), f32[16,64,128]{2,1,0:T(8,128)S(1)}, u32[]{:S(2)}, u32[]{:S(2)}) async-start(f32[16,64,128]{2,1,0:T(8,128)} %broadcast_in_dim.88), calls=%async_computation.24 | async-start | bytes 1048576 | tf_op jit(solution)/shard_map/all_to_all | solution.py:21
  445.9 20.9 %all-to-all-start.27 = ((f32[64,1,2048]{2,1,0:T(1,128)}), f32[64,1,2048]{2,1,0:T(1,128)S(1)}, u32[]{:S(2)}, u32[]{:S(2)}) async-start(f32[64,1,2048]{2,1,0:T(1,128)} %reshape.173), calls=%async_computation.27 | async-start | bytes 1048576 | tf_op jit(solution)/shard_map/all_to_all | solution.py:21
  475.3 7.4 %all-to-all-start.30 = ((f32[4,1,256]{2,1,0:T(1,128)}), f32[4,1,256]{2,1,0:T(1,128)S(1)}, u32[]{:S(2)}, u32[]{:S(2)}) async-start(f32[4,1,256]{2,1,0:T(1,128)} %reshape.175), calls=%async_computation.30 | async-start | bytes 8192 | tf_op jit(solution)/shard_map/all_to_all | solution.py:21
  482.7 15.3 %all-to-all-start.29 = ((f32[16,64,128]{2,1,0:T(8,128)}), f32[16,64,128]{2,1,0:T(8,128)S(1)}, u32[]{:S(2)}, u32[]{:S(2)}) async-start(f32[16,64,128]{2,1,0:T(8,128)} %copy.333), calls=%async_computation.29 | async-start | bytes 1048576 | tf_op jit(solution)/shard_map/all_to_all | solution.py:61
  498.1 18.2 %all-to-all-start.31 = ((f32[64,1,1024]{2,1,0:T(1,128)}), f32[64,1,1024]{2,1,0:T(1,128)S(1)}, u32[]{:S(2)}, u32[]{:S(2)}) async-start(f32[64,1,1024]{2,1,0:T(1,128)} %reshape.177), calls=%async_computation.31 | async-start | bytes 524288 | tf_op jit(solution)/shard_map/all_to_all | solution.py:21
  516.2 21.8 %all-to-all-start.28 = ((f32[16,64,128]{2,1,0:T(8,128)}), f32[16,64,128]{2,1,0:T(8,128)S(1)}, u32[]{:S(2)}, u32[]{:S(2)}) async-start(f32[16,64,128]{2,1,0:T(8,128)} %copy.331), calls=%async_computation.28 | async-start | bytes 1048576 | tf_op jit(solution)/shard_map/all_to_all | solution.py:61
  (6 other events, 50.9 us)
where the time goes:
time: 572 us; the launch traced here: 567 us
  waiting for transfers between devices  234 us (41%)
  starting transfers between devices  133 us (23%)
  blocking collectives  102 us (18%)
  local copies, waits for them, and re-layouts  40.5 us (7%)
  other arithmetic  26 us (5%)
  matrix products  15.9 us (3%)
  between operations  14.7 us (3%)
    all_to_all x20, waiting for transfers between devices, from_everyone(): lax.all_to_all(jnp.broadcast_to(value[None], (count, *value.shape)), axis...  176 us
    all_to_all x20, starting transfers between devices, from_everyone(): lax.all_to_all(jnp.broadcast_to(value[None], (count, *value.shape)), axis...  110 us
    all_to_all x8, blocking collectives, from_everyone(): lax.all_to_all(jnp.broadcast_to(value[None], (count, *value.shape)), axis...  86.1 us
    all_to_all x5, waiting for transfers between devices, sent_and_summed(): parts = lax.all_to_all(in_blocks(value, dim, count), axis, 0, 0, tiled=True)  58.4 us
    all_to_all x5, starting transfers between devices, sent_and_summed(): parts = lax.all_to_all(in_blocks(value, dim, count), axis, 0, 0, tiled=True)  23.5 us
    all_to_all x1, blocking collectives, sent_and_summed(): parts = lax.all_to_all(in_blocks(value, dim, count), axis, 0, 0, tiled=True)  16.2 us
    unnamed x40, local copies, waits for them, and re-layouts  15.5 us
    all_to_all x12, other arithmetic, from_everyone(): lax.all_to_all(jnp.broadcast_to(value[None], (count, *value.shape)), axis...  13.6 us
  transfers between devices with their start and end apart: 25, of which 25 were waited for; matrix products, arithmetic and copies ran while one was open for 7% of the time, Pallas kernels for 0%

commit v1 on v0

v1 whole, which is shorter than its diff:
```python
import jax
import jax.numpy as jnp
from jax import lax
from jax.experimental import pallas as pl
from jax.experimental.pallas import tpu as pltpu
from jax.sharding import PartitionSpec as P

G = 16
T = 4
RS = 4
F32 = jnp.float32
EXACT = lax.Precision.HIGHEST

COL_PEERS = [(dz, dc) for dz in (4, 3, 5, 2, 6, 1, 7) for dc in (0, 1)] + [(0, 1)]
ROW_PEERS = sorted(
    [(dy, dx) for dy in range(4) for dx in range(4) if (dy, dx) != (0, 0)],
    key=lambda d: -(min(d[0], 4 - d[0]) + min(d[1], 4 - d[1])),
)


def dot(a, b, dims):
    return lax.dot_general(a, b, (dims, ((), ())), precision=EXACT, preferred_element_type=F32)


def iota(shape, dim):
    return lax.broadcasted_iota(jnp.int32, shape, dim)


def kernel(
    coords, counts, damp, fa, fb, fc, data_hbm,
    out_a, out_b, out_c,
    data, cs0, cr0, rs0, rr0, cs1, cr1, rs1, rr1,
    cs2, cr2, rs2, rr2, cs3, cr3, rs3, rr3,
    cs4, cr4, rs4, rr4, cs5, cr5, rs5, rr5,
    cs6, cr6, rs6, rr6, cso, cro, rso, rro,
    va, vb, ga, gb, ta, tb, tat, da, db, jg, wa, wat, wb, wbt,
    data_sem, send_sem, recv_sem,
):
    p = lax.axis_index("row")
    q = lax.axis_index("col")
    col_of = []
    z, core = q // 2, q % 2
    for dz, dc in COL_PEERS:
        col_of.append(((z + dz) % 8) * 2 + (core + dc) % 2)
    row_of = []
    y, x = p // 4, p % 4
    for dy, dx in ROW_PEERS:
        row_of.append(((y + dy) % 4) * 4 + (x + dx) % 4)

    load = pltpu.make_async_copy(data_hbm, data, data_sem)
    load.start()

    barrier = pltpu.get_barrier_semaphore()
    for peer in col_of:
        pl.semaphore_signal(barrier, inc=1, device_id={"col": peer})
    for peer in row_of:
        pl.semaphore_signal(barrier, inc=1, device_id={"row": peer})

    def send(hop, axis, src, dst):
        me, peers, name = (q, col_of, "col") if axis == 0 else (p, row_of, "row")
        for peer in peers:
            pltpu.make_async_remote_copy(
                src_ref=src.at[peer],
                dst_ref=dst.at[me],
                send_sem=send_sem.at[hop, axis],
                recv_sem=recv_sem.at[hop, axis],
                device_id={name: peer},
            ).start()
        dst[me] = src[me]

    def wait(sem, ref):
        some = ref.at[pl.ds(0, G - 1)]
        pltpu.make_async_copy(some, some, sem).wait()

    def arrived(hop, axis, dst):
        wait(recv_sem.at[hop, axis], dst)

    lane = iota((1, 128), 1)

    def positions(coord_row, member):
        base = (member % 8) * 16
        here = lane - base
        val = jnp.zeros((1, 128), F32)
        for t in range(T):
            at = (here // RS == t) & (here >= 0)
            val = jnp.where(at, (coords[coord_row, t] * RS + here % RS).astype(F32), val)
        first = member // 8 == 0
        zero = jnp.zeros((1, 128), F32)
        return jnp.where(first, val, zero), jnp.where(first, zero, val)

    def depth_index(member):
        here = lane - member * 8
        val = jnp.zeros((1, 128), F32)
        for t in range(T):
            at = (here >= 0) & (here < 8) & (here % T == t)
            val = jnp.where(at, coords[2, t].astype(F32), val)
        return val

    zero_row = jnp.zeros((1, 128), F32)
    low, high = positions(0, q)
    info_col = jnp.concatenate([low, high, depth_index(q), zero_row], axis=0)
    low, high = positions(1, p)
    info_row = jnp.concatenate([low, high, depth_index(p), zero_row], axis=0)
    own = jnp.concatenate([jnp.zeros((64, 128), F32), jnp.pad(fc[...], ((0, 0), (0, 120)))], axis=0)
    own = jnp.transpose(own)[:8]
    for j in range(G):
        cs0[j, 0:4] = fa[4 * j:4 * j + 4]
        cs0[j, 4:8] = info_col
        cs0[j, 8:16] = own
        rs0[j, 0:4] = fb[4 * j:4 * j + 4]
        rs0[j, 4:8] = info_row

    pl.semaphore_wait(barrier, 2 * (G - 1))
    send(0, 0, cs0, cr0)
    send(0, 1, rs0, rr0)
    arrived(0, 0, cr0)
    arrived(0, 1, rr0)

    info_col = jnp.sum(cr0[:, 0:8], axis=0)
    info_row = jnp.sum(rr0[:, 0:8], axis=0)

    def matrices(info, w, wt):
        turned = jnp.transpose(info)
        for half in range(2):
            across = info[4 + half:5 + half].astype(jnp.int32)
            down = turned[:, 4 + half:5 + half].astype(jnp.int32)
            w[:, 128 * half:128 * half + 128] = (iota((64, 128), 0) == across).astype(F32)
            wt[128 * half:128 * half + 128] = (iota((128, 64), 1) == down).astype(F32)
        return turned

    matrices(info_col, wa, wat)
    turned = matrices(info_row, wb, wbt)
    k_here = info_col[6:7].astype(jnp.int32)
    k_there = turned[:, 6:7].astype(jnp.int32)
    down, across = iota((128, 128), 0), iota((128, 128), 1)
    slot_row = down % 8 < T
    own_index = (down // 8) * 128 + q * 8 + down % 8
    mix0 = (slot_row & (k_there == across + p * 128)).astype(F32)
    target = jnp.where(across % 8 < T, own_index, k_there)
    allowed = jnp.where(across % 8 < T, 1.0, slot_row.astype(F32))
    mix = (jnp.broadcast_to(k_here, (128, 128)) == target).astype(F32) * allowed

    def serve(wt, v, dst):
        s = dot(wt[...], v[...], ((1,), (0,)))
        dst[:, 0:16] = s.reshape(G, 16, 128)

    def mixed(m, tiles, dst):
        u = dot(m, tiles.reshape(128, 128), ((1,), (0,)))
        dst[:, 16:24] = u.reshape(G, 8, 128)

    for j in range(G):
        va[4 * j:4 * j + 4] = cr0[j, 0:4]
        vb[4 * j:4 * j + 4] = rr0[j, 0:4]
    serve(wat, va, cs1)
    send(1, 0, cs1, cr1)
    mixed(mix0, cr0[:, 8:16], rs1)
    serve(wbt, vb, rs1)
    send(1, 1, rs1, rr1)

    def unpack(src, dst):
        for t in range(T):
            for j in range(G):
                dst[t, 4 * j:4 * j + 4] = src[j, 4 * t:4 * t + 4]

    def pack(t, value, dst):
        for j in range(G):
            dst[j, 4 * t:4 * t + 4] = value[4 * j:4 * j + 4]

    def depth_of(src):
        total = jnp.sum(src[:, 16:24], axis=0)
        return total, jnp.transpose(total)

    arrived(1, 0, cr1)
    unpack(cr1, ta)
    arrived(1, 1, rr1)
    unpack(rr1, tb)
    total, turned_c = depth_of(rr1)
    depth = [jnp.broadcast_to(turned_c[64:128, t:t + 1], (64, 128)) for t in range(T)]
    load.wait()

    def gradients(t, values, cs, rs, cols):
        raw = dot(tb[t], values, ((1,), (1,)))
        pack(t, raw * depth[t], cs)
        pack(t, dot(ta[t] * depth[t], values, ((1,), (0,))), rs)
        col = jnp.sum(ta[t] * raw, axis=1, keepdims=True)
        lanes = iota((64, 128), 1)
        left = cols[0] + jnp.where(lanes == t, col, 0.0)
        right = cols[1] + jnp.where(lanes == t + T, col, 0.0)
        return left, right

    def depth_message(cols, cs):
        tile = jnp.transpose(jnp.concatenate(cols, axis=0))[:8]
        for j in range(G):
            cs[j, 16:24] = tile

    def live(t):
        return (t < counts[0]).astype(F32)

    cols = (jnp.zeros((64, 128), F32), jnp.zeros((64, 128), F32))
    for t in range(T):
        tat[t] = jnp.transpose(ta[t])
        model = dot(tat[t], tb[t] * depth[t], ((1,), (0,)))
        values = (data[t].astype(F32) - model) * live(t)
        cols = gradients(t, values, cs2, rs2, cols)
    depth_message(cols, cs2)
    send(2, 0, cs2, cr2)
    send(2, 1, rs2, rr2)

    def fold(w, src, v):
        v[...] = dot(w[...], src.reshape(256, 128), ((1,), (0,)))

    half_mask = ((down % 8 < T) == (across < 64)).astype(F32)

    def masked(src):
        return src[:, 16:24].reshape(128, 128) * half_mask

    arrived(2, 0, cr2)
    fold(wa, cr2[:, 0:16], ga)
    serve(wat, ga, cs3)
    send(3, 0, cs3, cr3)
    arrived(2, 1, rr2)
    fold(wb, rr2[...], gb)
    serve(wbt, gb, rs3)
    mixed(mix, masked(cr2), rs3)
    send(3, 1, rs3, rr3)
    arrived(3, 0, cr3)
    unpack(cr3, da)
    arrived(3, 1, rr3)
    unpack(rr3, db)
    total_g, turned_g = depth_of(rr3)

    def jacobian(t, turned_u):
        du = jnp.broadcast_to(turned_u[64:128, t:t + 1], (64, 128))
        right = db[t] * depth[t] + tb[t] * du
        left = jnp.transpose(da[t])
        return dot(left, tb[t] * depth[t], ((1,), (0,))) + dot(tat[t], right, ((1,), (0,)))

    def norm(value):
        return jnp.sum(value, axis=(0, 1), keepdims=True)

    cols = (jnp.zeros((64, 128), F32), jnp.zeros((64, 128), F32))
    squares = jnp.zeros((128, 128), F32)
    for t in range(T):
        values = jacobian(t, turned_g) * live(t)
        jg[t] = values
        squares = squares + values * values
        cols = gradients(t, values, cs4, rs4, cols)
    own_g = total_g[:, 0:64]
    g_part = norm(ga[...] * ga[...]) + norm(gb[...] * gb[...]) + norm(own_g * own_g)
    j_part = norm(squares)
    tile = jnp.transpose(jnp.concatenate(cols, axis=0))[:8]
    row8, lane8 = iota((8, 128), 0), iota((8, 128), 1)
    tile = jnp.where((row8 == 0) & (lane8 >= 64), g_part, tile)
    tile = jnp.where((row8 == 1) & (lane8 >= 64), j_part, tile)
    for j in range(G):
        cs4[j, 16:24] = tile
    send(4, 0, cs4, cr4)
    send(4, 1, rs4, rr4)

    arrived(4, 0, cr4)
    fold(wa, cr4[:, 0:16], va)
    serve(wat, va, cs5)
    send(5, 0, cs5, cr5)
    group = jnp.sum(cr4[:, 16:24], axis=0)
    arrived(4, 1, rr4)
    fold(wb, rr4[...], vb)
    serve(wbt, vb, rs5)
    u = dot(mix, masked(cr4), ((1,), (0,)))
    up = (across >= 64) & (down % 8 >= T)
    u = jnp.where(up & (down % 8 == 4), jnp.broadcast_to(group[0:1, 127:128], (128, 128)), u)
    u = jnp.where(up & (down % 8 == 5), jnp.broadcast_to(group[1:2, 127:128], (128, 128)), u)
    rs5[:, 16:24] = u.reshape(G, 8, 128)
    send(5, 1, rs5, rr5)

    for j in range(G):
        cso[j, 0:4] = ga[4 * j:4 * j + 4]
        cso[j, 4:8] = va[4 * j:4 * j + 4]
        rso[j, 0:4] = gb[4 * j:4 * j + 4]
        rso[j, 4:8] = vb[4 * j:4 * j + 4]
    send(6, 0, cso, cro)
    send(6, 1, rso, rro)

    arrived(5, 0, cr5)
    unpack(cr5, da)
    arrived(5, 1, rr5)
    unpack(rr5, db)
    total_w, turned_w = depth_of(rr5)
    lam = damp[0]
    g_norm = total_w[4:5, 127:128]
    j_norm = total_w[5:6, 127:128]
    alpha0 = g_norm / (j_norm + lam * g_norm)

    def residual_of(g, w):
        return g - alpha0 * (w + lam * g)

    own_w = total_w[:, 0:64]
    r_a = residual_of(ga[...], va[...])
    r_b = residual_of(gb[...], vb[...])
    r_c = residual_of(own_g, own_w)
    rr_part = norm(r_a * r_a) + norm(r_b * r_b) + norm(r_c * r_c)
    rg_part = norm(r_a * ga[...]) + norm(r_b * gb[...]) + norm(r_c * own_g)
    square = jnp.zeros((128, 128), F32)
    cross = jnp.zeros((128, 128), F32)
    for t in range(T):
        jw = jacobian(t, turned_w) * live(t)
        jr = residual_of(jg[t], jw)
        square = square + jr * jr
        cross = cross + jr * jg[t]

    parts = (rr_part, rg_part, norm(square), norm(cross))
    tile = jnp.zeros((8, 128), F32)
    for i, part in enumerate(parts):
        tile = jnp.where(row8 == i, part, tile)
    for j in range(G):
        cs6[j] = tile
    send(7, 0, cs6, cr6)
    arrived(7, 0, cr6)
    tile = jnp.sum(cr6[...], axis=0)
    for j in range(G):
        rs6[j] = tile
    send(7, 1, rs6, rr6)

    arrived(6, 0, cro)
    arrived(6, 1, rro)
    arrived(7, 1, rr6)
    tile = jnp.sum(rr6[...], axis=0)
    r_norm, r_g, jr_norm, jr_jg = [tile[i:i + 1, 0:1] for i in range(4)]
    beta = r_norm / g_norm
    curve = (
        jr_norm + lam * r_norm
        + 2.0 * beta * (jr_jg + lam * r_g)
        + beta * beta * (j_norm + lam * g_norm)
    )
    alpha1 = r_norm / curve

    def step(g, w):
        return alpha0 * g + alpha1 * (residual_of(g, w) + beta * g)

    for j in range(G):
        out_a[4 * j:4 * j + 4] = step(cro[j, 0:4], cro[j, 4:8])
        out_b[4 * j:4 * j + 4] = step(rro[j, 0:4], rro[j, 4:8])
    out_c[...] = step(turned_g[0:64, 0:8], turned_w[0:64, 0:8])

    for hop, axis, src in (
        (0, 0, cs0), (0, 1, rs0), (1, 0, cs1), (1, 1, rs1), (2, 0, cs2), (2, 1, rs2),
        (3, 0, cs3), (3, 1, rs3), (4, 0, cs4), (4, 1, rs4), (5, 0, cs5), (5, 1, rs5),
        (6, 0, cso), (6, 1, rso), (7, 0, cs6), (7, 1, rs6),
    ):
        wait(send_sem.at[hop, axis], src)


def per_device(
    tile_data, tile_coords, tile_counts, factor_rows, factor_cols, factor_depth, damping
):
    vmem = pl.BlockSpec(memory_space=pltpu.VMEM)
    smem = pl.BlockSpec(memory_space=pltpu.SMEM)
    rows = lambda n: pltpu.VMEM((G, n, 128), F32)
    pair = lambda n: [rows(n), rows(n)]
    return pl.pallas_call(
        kernel,
        out_shape=(
            jax.ShapeDtypeStruct((64, 128), F32),
            jax.ShapeDtypeStruct((64, 128), F32),
            jax.ShapeDtypeStruct((64, 8), F32),
        ),
        in_specs=[smem, smem, smem, vmem, vmem, vmem, pl.BlockSpec(memory_space=pl.ANY)],
        out_specs=(vmem, vmem, vmem),
        scratch_shapes=[
            pltpu.VMEM((T, 128, 128), jnp.bfloat16),
            *pair(16), *pair(8),
            *pair(16), *pair(24),
            *pair(24), *pair(16),
            *pair(16), *pair(24),
            *pair(24), *pair(16),
            *pair(16), *pair(24),
            *pair(8), *pair(8),
            *pair(8), *pair(8),
            *[pltpu.VMEM((64, 128), F32)] * 4,
            *[pltpu.VMEM((T, 64, 128), F32)] * 2,
            pltpu.VMEM((T, 128, 64), F32),
            *[pltpu.VMEM((T, 64, 128), F32)] * 2,
            pltpu.VMEM((T, 128, 128), F32),
            pltpu.VMEM((64, 256), F32), pltpu.VMEM((256, 64), F32),
            pltpu.VMEM((64, 256), F32), pltpu.VMEM((256, 64), F32),
            pltpu.SemaphoreType.DMA,
            pltpu.SemaphoreType.DMA((8, 2)),
            pltpu.SemaphoreType.DMA((8, 2)),
        ],
        compiler_params=pltpu.CompilerParams(collective_id=0, has_side_effects=True),
        name="gauss_newton",
    )(
        tile_coords, tile_counts, damping.reshape(1),
        factor_rows, factor_cols, factor_depth, tile_data,
    )


def solution(mesh):
    both = ("row", "col")
    flip = ("col", "row")
    return jax.shard_map(
        per_device,
        mesh=mesh,
        in_specs=(
            P(both, None, None), P(None, both), P(both),
            P(None, both), P(None, flip), P(None, both), P(),
        ),
        out_specs=(P(None, both), P(None, flip), P(None, both)),
        check_vma=False,
    )
```

time: 572 us -> 69.9 us (0.12)
  waiting for transfers between devices: 234 us -> 0 us
  starting transfers between devices: 133 us -> 0 us
  blocking collectives: 102 us -> 0 us
  Pallas kernels: 0 us -> 64.1 us
  local copies, waits for them, and re-layouts: 40.5 us -> 3.51 us
  other arithmetic: 26 us -> 0 us
  matrix products: 15.9 us -> 0 us
  between operations: 14.7 us -> 1.97 us
    all_to_all x25 -> x0, waiting for transfers between devices: 234 us -> none  [the longest x20 176 us: from_everyone(): lax.all_to_all(jnp.broadcast_to(value[None], (count, *value.shape)), axis...]
    all_to_all x25 -> x0, starting transfers between devices: 133 us -> none  [the longest x20 110 us: from_everyone(): lax.all_to_all(jnp.broadcast_to(value[None], (count, *value.shape)), axis...]
    all_to_all x9 -> x0, blocking collectives: 102 us -> none  [the longest x8 86.1 us: from_everyone(): lax.all_to_all(jnp.broadcast_to(value[None], (count, *value.shape)), axis...]
    pallas_call x0 -> x1, Pallas kernels: none -> 64.1 us  [per_device(): pl.pallas_call(kernel, out_shape=(jax.ShapeDtypeStruct((64, 128), F32), j...]
    dot_general x24 -> x0, matrix products: 15.9 us -> none  [the longest x6 3.64 us: pick_rows(): return jnp.einsum('tq,rqa->tra', onehot, shaped, precision=exact_precision)]
    all_to_all x12 -> x0, other arithmetic: 13.6 us -> none  [from_everyone(): lax.all_to_all(jnp.broadcast_to(value[None], (count, *value.shape)), axis...]
    unnamed x40 -> x9, local copies, waits for them, and re-layouts: 15.5 us -> 2.09 us
    broadcast_in_dim x22 -> x0, local copies, waits for them, and re-layouts: 10.1 us -> none  [from_everyone(): jnp.broadcast_to(value[None], (count, *value.shape))]
  transfers between devices with their start and end apart: 25 -> 0, of which waited for: 25 -> 0; matrix products, arithmetic and copies ran while one was open for 7% -> 0% of each run, Pallas kernels for 0% -> 0%
where the time goes in v1:
time: 69.9 us; the launch traced here: 69.6 us
  Pallas kernels  64.1 us (92%)
  local copies, waits for them, and re-layouts  3.51 us (5%)
  between operations  1.97 us (3%)
    pallas_call x1, Pallas kernels, per_device(): pl.pallas_call(kernel, out_shape=(jax.ShapeDtypeStruct((64, 128), F32), j...  64.1 us
    unnamed x9, local copies, waits for them, and re-layouts  2.09 us
    pallas_call x1, local copies, waits for them, and re-layouts, per_device(): pl.pallas_call(kernel, out_shape=(jax.ShapeDtypeStruct((64, 128), F32), j...  1.42 us

profile of v1, /device:TPU:1, one launch (start us, length us, event | category | flops | bytes accessed | tf_op | source)
XLA Modules:
  0.0 69.6 jit_solution(10055937650096006755)
XLA Ops:
  0.6 0.0 copy-start.2
  1.9 0.0 copy-done.2
  2.0 0.7 %copy.10.fc = f32[64,8]{1,0:T(8,128)} copy(f32[64,8]{0,1:T(8,128)S(1)} %copy-done.2) | data formatting | bytes 4096 | tf_op args[5]
  2.7 64.1 %gauss_newton.1 = (f32[64,128]{1,0:T(8,128)}, f32[64,128]{1,0:T(8,128)}, f32[64,8]{1,0:T(8,128)}) custom-call(s32[3,4]{1,0:T(4,128)} %coords.1, s32[1]{0:T(128)S(6)} %copy.14.counts, f32[1]{0:T(128)} %bitcast.1.damp, f32[64,128]{1,0:T(8,128)} %fa.1, f32[64,128]{1,0:T(8,128)} %fb.1, f32[64,8]{1,0:T(8,128)} %copy.10.fc, bf16[4,128,128]{2,1,0:T(8,128)(2,1)} %data_hbm.1), custom_call_target="tpu_custom_call" | custom-call | tf_op jit(solution)/shard_map/gauss_newton/pallas_call | solution.py:359
  66.8 0.0 copy-start.1
  66.8 1.4 %copy.11 = f32[64,8]{0,1:T(8,128)} copy(f32[64,8]{1,0:T(8,128)} %get-tuple-element.5) | data formatting | bytes 4096 | tf_op jit(solution)/shard_map/gauss_newton/pallas_call | solution.py:359
  68.2 0.0 copy-done.1
  68.2 0.0 copy-start
  68.2 0.6 copy.16
  68.8 0.2 copy-done
  69.0 0.6 copy.17
Async XLA Ops:
  0.6 1.3 %copy-start.2 = (f32[64,8]{0,1:T(8,128)S(1)}, f32[64,8]{0,1:T(8,128)}, u32[]{:S(2)}) copy-start(f32[64,8]{0,1:T(8,128)} %param.12) | copy-start | bytes 6148
  66.8 1.4 %copy-start.1 = (f32[64,128]{1,0:T(8,128)S(1)}, f32[64,128]{1,0:T(8,128)}, u32[]{:S(2)}) copy-start(f32[64,128]{1,0:T(8,128)} %get-tuple-element.9) | copy-start | bytes 98308
  68.2 0.8 %copy-start = (f32[64,128]{1,0:T(8,128)S(1)}, f32[64,128]{1,0:T(8,128)}, u32[]{:S(2)}) copy-start(f32[64,128]{1,0:T(8,128)} %get-tuple-element.10) | copy-start | bytes 98308

commit v2 on v1

v2 whole, which is shorter than its diff:
```python
import jax
import jax.numpy as jnp
from jax import lax
from jax.experimental import pallas as pl
from jax.experimental.pallas import tpu as pltpu
from jax.sharding import PartitionSpec as P

G = 16
T = 4
RS = 4
F32 = jnp.float32
BF16 = jnp.bfloat16

COL_PEERS = [(dz, dc) for dz in (4, 3, 5, 2, 6, 1, 7) for dc in (0, 1)] + [(0, 1)]
ROW_PEERS = sorted(
    [(dy, dx) for dy in range(4) for dx in range(4) if (dy, dx) != (0, 0)],
    key=lambda d: -(min(d[0], 4 - d[0]) + min(d[1], 4 - d[1])),
)

EXCHANGES = (
    ("a_slices", 0, 8), ("a_depth", 0, 4), ("b_slices", 1, 8),
    ("a_slots", 0, 16), ("b_slots", 1, 16), ("c_slots", 1, 8),
    ("ga_in", 0, 16), ("gc_in", 0, 4), ("gb_in", 1, 16),
    ("ga_out", 0, 16), ("gb_out", 1, 16), ("gc_out", 1, 8),
    ("wa_in", 0, 16), ("wc_in", 0, 4), ("wb_in", 1, 16),
    ("wa_out", 0, 16), ("wb_out", 1, 16), ("wc_out", 1, 8),
    ("a_put", 0, 8), ("b_put", 1, 8),
    ("sum_col", 0, 1), ("sum_row", 1, 1),
)
INDEX = {name: i for i, (name, _, _) in enumerate(EXCHANGES)}


def mm(a, b, rhs_dim=0):
    return lax.dot_general(a, b, (((1,), (rhs_dim,)), ((), ())), preferred_element_type=F32)


def two(x):
    high = x.astype(BF16)
    return high, (x - high.astype(F32)).astype(BF16)


def three(x, axis=0):
    high = x.astype(BF16)
    rest = x - high.astype(F32)
    mid = rest.astype(BF16)
    low = (rest - mid.astype(F32)).astype(BF16)
    return jnp.concatenate([high, mid, low], axis=axis)


def mm_two(left, right, rhs_dim=0):
    rows = left.shape[0] // 2
    high, low = right
    both = mm(left, high, rhs_dim)
    return both[:rows] + both[rows:] + mm(left[:rows], low, rhs_dim)


def iota(shape, dim):
    return lax.broadcasted_iota(jnp.int32, shape, dim)


def kernel(coords_hbm, counts_hbm, damp_hbm, fa_hbm, fb_hbm, fc_hbm, data_hbm, *refs):
    out_a, out_b, out_c = refs[:3]
    refs = refs[3:]
    n = len(EXCHANGES)
    outbox, inbox = refs[:n], refs[n:2 * n]
    (
        coords, counts, damp, fa, fb, fc, data,
        va, vb, ga, gb, ta, tb, da, db, jg,
        at2, tb2, tac2, bc_high, bc_low, left, xc,
        wa, wb, wat, wbt, mix, load_sem, send_sem, recv_sem,
    ) = refs[2 * n:]
    p = lax.axis_index("row")
    q = lax.axis_index("col")
    z, core = q // 2, q % 2
    col_of = [((z + dz) % 8) * 2 + (core + dc) % 2 for dz, dc in COL_PEERS]
    y, x = p // 4, p % 4
    row_of = [((y + dy) % 4) * 4 + (x + dx) % 4 for dy, dx in ROW_PEERS]

    barrier = pltpu.get_barrier_semaphore()
    for peer in col_of:
        pl.semaphore_signal(barrier, inc=1, device_id={"col": peer})
    for peer in row_of:
        pl.semaphore_signal(barrier, inc=1, device_id={"row": peer})

    loads = [
        pltpu.make_async_copy(src, dst, load_sem.at[i])
        for i, (src, dst) in enumerate((
            (coords_hbm, coords), (counts_hbm, counts), (damp_hbm, damp),
            (fa_hbm, fa), (fb_hbm, fb), (fc_hbm, fc), (data_hbm, data),
        ))
    ]
    for load in loads:
        load.start()

    def box(name):
        return outbox[INDEX[name]], inbox[INDEX[name]]

    def send(name):
        i = INDEX[name]
        me, peers, axis = ((q, col_of, "col"), (p, row_of, "row"))[EXCHANGES[i][1]]
        src, dst = outbox[i], inbox[i]
        for peer in peers:
            pltpu.make_async_remote_copy(
                src_ref=src.at[peer],
                dst_ref=dst.at[me],
                send_sem=send_sem.at[i],
                recv_sem=recv_sem.at[i],
                device_id={axis: peer},
            ).start()
        dst[me] = src[me]

    def wait(sem, ref):
        some = ref.at[pl.ds(0, G - 1)]
        pltpu.make_async_copy(some, some, sem).wait()

    def arrived(name):
        i = INDEX[name]
        wait(recv_sem.at[i], inbox[i])
        return inbox[i]

    lane = iota((1, 128), 1)
    zero_row = jnp.zeros((1, 128), F32)

    def positions(coord_row, member):
        here = lane - (member % 8) * 16
        val = zero_row
        for t in range(T):
            at = (here >= RS * t) & (here < RS * t + RS)
            val = jnp.where(at, (coords[coord_row, t] * RS + here - RS * t).astype(F32), val)
        first = member // 8 == 0
        return jnp.where(first, val, zero_row), jnp.where(first, zero_row, val)

    def depth_index(member):
        here = lane - member * 8
        val = zero_row
        for t in range(T):
            at = (here == t) | (here == t + T)
            val = jnp.where(at, coords[2, t].astype(F32), val)
        return val

    loads[0].wait()
    first, second = positions(0, q)
    info_col = jnp.concatenate([first, second, depth_index(q), zero_row], axis=0)
    first, second = positions(1, p)
    info_row = jnp.concatenate([first, second, depth_index(p), zero_row], axis=0)
    for load in loads[3:6]:
        load.wait()
    own = jnp.concatenate([fc[0:4], fc[4:8]], axis=1)
    a_slices, a_depth, b_slices = box("a_slices")[0], box("a_depth")[0], box("b_slices")[0]
    for j in range(G):
        a_slices[j, 0:4] = fa[4 * j:4 * j + 4]
        a_slices[j, 4:8] = info_col
        a_depth[j] = own
        b_slices[j, 0:4] = fb[4 * j:4 * j + 4]
        b_slices[j, 4:8] = info_row

    pl.semaphore_wait(barrier, 2 * (G - 1))
    send("a_slices")
    send("b_slices")
    send("a_depth")

    def across_of(info):
        return jnp.concatenate([info[4:5], info[5:6]], axis=1).astype(jnp.int32)

    def back_matrix(info, dst):
        turned = jnp.transpose(info).astype(jnp.int32)
        lanes = iota((128, 64), 1)
        for half in range(2):
            w = (lanes == turned[:, 4 + half:5 + half]).astype(BF16)
            dst[128 * half:128 * half + 128] = jnp.concatenate([w, w, w], axis=1)
        return turned

    def serve(w, v, name):
        s = mm(w[...], three(v))
        box(name)[0][...] = s.reshape(G, 16, 128)
        send(name)

    def stacked(src):
        for j in range(G):
            xc[4 * j:4 * j + 4] = src[j]
        return xc[...]

    src = arrived("b_slices")
    info_row = jnp.sum(src[...], axis=0)
    turned = back_matrix(info_row, wbt)
    for j in range(G):
        vb[4 * j:4 * j + 4] = src[j, 0:4]
    serve(wbt, vb[...], "b_slots")
    src = arrived("a_slices")
    info_col = jnp.sum(src[...], axis=0)
    back_matrix(info_col, wat)
    for j in range(G):
        va[4 * j:4 * j + 4] = src[j, 0:4]
    serve(wat, va[...], "a_slots")
    src = arrived("a_depth")
    k_there = turned[:, 6:7]
    down, half = iota((128, 64), 0), iota((128, 64), 1)
    column = p * 128 + (half // 4) * 8 + half % 4
    slot_row = (down % 8 < T).astype(F32)
    pick = [
        ((k_there == column + 4 * i).astype(F32) * slot_row).astype(BF16) for i in range(2)
    ]
    pick = jnp.concatenate(pick, axis=0)
    both = mm(jnp.concatenate([pick, pick, pick], axis=1), three(stacked(src)))
    c_out = box("c_slots")[0]
    c_out[...] = (pltpu.roll(both[:128], 64, 1) + both[128:]).reshape(G, 8, 128)
    send("c_slots")

    wa[...] = (iota((64, 256), 0) == across_of(info_col)).astype(BF16)
    wb[...] = (iota((64, 256), 0) == across_of(info_row)).astype(BF16)

    spread = (iota((128, 64), 0) == (half // 4) * 8 + half % 4).astype(BF16)
    k_tiles = jnp.broadcast_to(info_col[6:7], (8, 128))
    k_lane = mm(three(k_tiles, 1), jnp.concatenate([spread, spread, spread], axis=0))
    k_lane = k_lane[0:1].astype(jnp.int32)
    own_index = (down // 8) * 128 + q * 8 + down % 8
    to_own = (k_lane == own_index).astype(BF16)
    to_slot = ((k_lane == k_there).astype(F32) * slot_row).astype(BF16)
    to_both = jnp.concatenate([to_own, to_slot], axis=0)
    mix[...] = jnp.concatenate([to_both, to_both, to_both], axis=1)

    def unpack(src, dst):
        for t in range(T):
            for j in range(G):
                dst[t, 4 * j:4 * j + 4] = src[j, 4 * t:4 * t + 4]

    def pack(t, value, dst):
        for j in range(G):
            dst[j, 4 * t:4 * t + 4] = value[4 * j:4 * j + 4]

    def columns(turned):
        return [jnp.broadcast_to(turned[64:128, t:t + 1], (64, 128)) for t in range(T)]

    src = arrived("b_slots")
    unpack(src, tb)
    for t in range(T):
        high, low = two(tb[t])
        tb2[t, 0:64] = high
        tb2[t, 64:128] = low
    src = arrived("c_slots")
    depth = columns(jnp.transpose(jnp.sum(src[...], axis=0)))
    for t in range(T):
        bc_high[t], bc_low[t] = two(tb[t] * depth[t])
    for load in (loads[1], loads[2], loads[6]):
        load.wait()
    src = arrived("a_slots")
    unpack(src, ta)

    def live(t):
        return (t < counts[0]).astype(F32)

    def gradients(all_values, name):
        ga_out, gc_out, gb_out = [box(name + mode + "_in")[0] for mode in "acb"]
        parts = [two(values) for values in all_values]
        cols = jnp.zeros((64, 128), F32)
        lanes = iota((64, 128), 1)
        for t in range(T):
            raw = mm_two(tb2[t], parts[t], 1)
            pack(t, raw * depth[t], ga_out)
            col = jnp.sum(ta[t] * raw, axis=1, keepdims=True)
            cols = jnp.where(lanes == t, col, cols)
        send(name + "a_in")
        for t in range(T):
            pack(t, mm_two(tac2[t], parts[t]), gb_out)
        send(name + "b_in")
        tile = jnp.transpose(jnp.concatenate([cols, jnp.zeros((64, 128), F32)], axis=0))[:4]
        return tile, gc_out

    all_values = []
    for t in range(T):
        high, low = two(jnp.transpose(ta[t]))
        at2[t, 0:128] = high
        at2[t, 128:256] = low
        high, low = two(ta[t] * depth[t])
        tac2[t, 0:64] = high
        tac2[t, 64:128] = low
        model = mm_two(at2[t], (bc_high[t], bc_low[t]))
        all_values.append((data[t].astype(F32) - model) * live(t))
    tile, gc_out = gradients(all_values, "g")
    for j in range(G):
        gc_out[j] = tile
    send("gc_in")
    for t in range(T):
        left[t, :, 64:128] = at2[t]

    def fold(w, src, v):
        rows = src.reshape(256, 128)
        parts = three(rows)
        v[...] = mm(w[...], parts[0:256]) + (mm(w[...], parts[256:512]) + mm(w[...], parts[512:768]))
        return v[...]

    def blend(src):
        both = mm(mix[...], three(stacked(src)))
        return jnp.where(iota((128, 128), 1) < 64, both[:128], pltpu.roll(both[128:], 64, 1))

    src = arrived("gb_in")
    serve(wbt, fold(wb, src[...], gb), "gb_out")
    src = arrived("ga_in")
    serve(wat, fold(wa, src[...], ga), "ga_out")
    src = arrived("gc_in")
    box("gc_out")[0][...] = blend(src).reshape(G, 8, 128)
    send("gc_out")

    def direction(name):
        src = arrived(name + "b_out")
        unpack(src, db)
        src = arrived(name + "c_out")
        total = jnp.sum(src[...], axis=0)
        du = columns(jnp.transpose(total))
        rights = []
        for t in range(T):
            high, low = two(db[t] * depth[t] + tb[t] * du[t])
            rights.append((
                jnp.concatenate([bc_high[t], high], axis=0),
                jnp.concatenate([bc_low[t], low], axis=0),
            ))
        src = arrived(name + "a_out")
        unpack(src, da)
        products = []
        for t in range(T):
            high, low = two(jnp.transpose(da[t]))
            left[t, 0:128, 0:64] = high
            left[t, 128:256, 0:64] = low
            products.append(mm_two(left[t], rights[t]) * live(t))
        return total, products

    def norm(value):
        return jnp.sum(value, axis=(0, 1), keepdims=True)

    total_g, products = direction("g")
    tile, gc_out = gradients(products, "w")
    squares = jnp.zeros((128, 128), F32)
    for t in range(T):
        jg[t] = products[t]
        squares = squares + products[t] * products[t]
    own_g = total_g[:, 0:64]
    g_part = norm(ga[...] * ga[...]) + norm(gb[...] * gb[...]) + norm(own_g * own_g)
    j_part = norm(squares)
    row4, lane4 = iota((4, 128), 0), iota((4, 128), 1)
    tile = jnp.where((row4 == 0) & (lane4 >= 64), g_part, tile)
    tile = jnp.where((row4 == 1) & (lane4 >= 64), j_part, tile)
    for j in range(G):
        gc_out[j] = tile
    send("wc_in")

    src = arrived("wb_in")
    serve(wbt, fold(wb, src[...], vb), "wb_out")
    src = arrived("wa_in")
    serve(wat, fold(wa, src[...], va), "wa_out")
    src = arrived("wc_in")
    group = jnp.sum(src[...], axis=0)
    u = blend(src)
    down, across = iota((128, 128), 0), iota((128, 128), 1)
    u = jnp.where(across >= 64, jnp.where(down % 8 == 4, group[0:1, 127:128], u), u)
    u = jnp.where(across >= 64, jnp.where(down % 8 == 5, group[1:2, 127:128], u), u)
    box("wc_out")[0][...] = u.reshape(G, 8, 128)
    send("wc_out")

    a_put, b_put = box("a_put")[0], box("b_put")[0]
    for j in range(G):
        a_put[j, 0:4] = ga[4 * j:4 * j + 4]
        a_put[j, 4:8] = va[4 * j:4 * j + 4]
        b_put[j, 0:4] = gb[4 * j:4 * j + 4]
        b_put[j, 4:8] = vb[4 * j:4 * j + 4]
    send("a_put")
    send("b_put")

    total_w, products = direction("w")
    lam = damp[0]
    g_norm = total_w[4:5, 127:128]
    j_norm = total_w[5:6, 127:128]
    alpha0 = g_norm / (j_norm + lam * g_norm)

    def residual_of(g, w):
        return g - alpha0 * (w + lam * g)

    own_w = total_w[:, 0:64]
    r_a = residual_of(ga[...], va[...])
    r_b = residual_of(gb[...], vb[...])
    r_c = residual_of(own_g, own_w)
    rr_part = norm(r_a * r_a + r_b * r_b) + norm(r_c * r_c)
    rg_part = norm(r_a * ga[...] + r_b * gb[...]) + norm(r_c * own_g)
    square = jnp.zeros((128, 128), F32)
    cross = jnp.zeros((128, 128), F32)
    for t in range(T):
        jr = residual_of(jg[t], products[t])
        square = square + jr * jr
        cross = cross + jr * jg[t]

    parts = (rr_part, rg_part, norm(square), norm(cross))
    row = zero_row
    for i, part in enumerate(parts):
        row = jnp.where(lane // 32 == i, part, row)
    out = box("sum_col")[0]
    for j in range(G):
        out[j] = row
    send("sum_col")
    src = arrived("sum_col")
    row = jnp.sum(src[...], axis=0)
    out = box("sum_row")[0]
    for j in range(G):
        out[j] = row
    send("sum_row")
    src_a = arrived("a_put")
    src_b = arrived("b_put")
    src = arrived("sum_row")
    row = jnp.sum(src[...], axis=0)
    r_norm, r_g, jr_norm, jr_jg = [row[:, 32 * i:32 * i + 1] for i in range(4)]
    beta = r_norm / g_norm
    curve = (
        jr_norm + lam * r_norm
        + 2.0 * beta * (jr_jg + lam * r_g)
        + beta * beta * (j_norm + lam * g_norm)
    )
    alpha1 = r_norm / curve

    def step(g, w):
        return alpha0 * g + alpha1 * (residual_of(g, w) + beta * g)

    for j in range(G):
        out_a[4 * j:4 * j + 4] = step(src_a[j, 0:4], src_a[j, 4:8])
        out_b[4 * j:4 * j + 4] = step(src_b[j, 0:4], src_b[j, 4:8])
    out_c[...] = step(own_g, own_w)
    for i in range(n):
        wait(send_sem.at[i], outbox[i])


def put(a, b, c, x, y, z):
    x[...] = a[...]
    y[...] = b[...]
    z[...] = c[...]


def per_device(
    tile_data, tile_coords, tile_counts, factor_rows, factor_cols, factor_depth, damping
):
    vmem = pl.BlockSpec(memory_space=pltpu.VMEM)
    boxes = [pltpu.VMEM((G, rows, 128), F32) for _, _, rows in EXCHANGES]
    blocks = ((64, 128), (64, 128), (8, 64))
    steps = pl.pallas_call(
        kernel,
        out_shape=tuple(pltpu.VMEM(block, F32) for block in blocks),
        in_specs=[pl.BlockSpec(memory_space=pltpu.HBM)] * 7,
        out_specs=(vmem, vmem, vmem),
        scratch_shapes=[
            *boxes, *boxes,
            pltpu.SMEM((3, T), jnp.int32), pltpu.SMEM((1,), jnp.int32), pltpu.SMEM((1,), F32),
            pltpu.VMEM((64, 128), F32), pltpu.VMEM((64, 128), F32), pltpu.VMEM((8, 64), F32),
            pltpu.VMEM((T, 128, 128), BF16),
            *[pltpu.VMEM((64, 128), F32)] * 4,
            *[pltpu.VMEM((T, 64, 128), F32)] * 4,
            pltpu.VMEM((T, 128, 128), F32),
            pltpu.VMEM((T, 256, 64), BF16),
            pltpu.VMEM((T, 128, 128), BF16), pltpu.VMEM((T, 128, 128), BF16),
            pltpu.VMEM((T, 64, 128), BF16), pltpu.VMEM((T, 64, 128), BF16),
            pltpu.VMEM((T, 256, 128), BF16),
            pltpu.VMEM((64, 128), F32),
            pltpu.VMEM((64, 256), BF16), pltpu.VMEM((64, 256), BF16),
            pltpu.VMEM((256, 192), BF16), pltpu.VMEM((256, 192), BF16),
            pltpu.VMEM((256, 192), BF16),
            pltpu.SemaphoreType.DMA((7,)),
            pltpu.SemaphoreType.DMA((len(EXCHANGES),)),
            pltpu.SemaphoreType.DMA((len(EXCHANGES),)),
        ],
        compiler_params=pltpu.CompilerParams(collective_id=0, has_side_effects=True),
        name="gauss_newton",
    )(
        tile_coords, tile_counts, damping.reshape(1),
        factor_rows, factor_cols, factor_depth.T, tile_data,
    )
    step_a, step_b, step_c = pl.pallas_call(
        put,
        out_shape=tuple(jax.ShapeDtypeStruct(block, F32) for block in blocks),
        in_specs=[vmem, vmem, vmem],
        out_specs=(vmem, vmem, vmem),
        name="put",
    )(*[pltpu.with_memory_space_constraint(step, pltpu.VMEM) for step in steps])
    return step_a, step_b, step_c.T


def solution(mesh):
    both = ("row", "col")
    flip = ("col", "row")
    return jax.shard_map(
        per_device,
        mesh=mesh,
        in_specs=(
            P(both, None, None), P(None, both), P(both),
            P(None, both), P(None, flip), P(None, both), P(),
        ),
        out_specs=(P(None, both), P(None, flip), P(None, both)),
        check_vma=False,
    )
```

time: 69.9 us -> 58.8 us (0.84)
  Pallas kernels: 64.1 us -> 56.7 us
  local copies, waits for them, and re-layouts: 3.51 us -> 0 us
    pallas_call x1 -> x2, Pallas kernels: 64.1 us -> 56.7 us  [the longest x1 56.1 us: per_device(): pl.pallas_call(kernel, out_shape=tuple((pltpu.VMEM(block, F32) for block...]
    unnamed x9 -> x0, local copies, waits for them, and re-layouts: 2.09 us -> none
    pallas_call x1 -> x0, local copies, waits for them, and re-layouts: 1.42 us -> none  [per_device(): pl.pallas_call(kernel, out_shape=(jax.ShapeDtypeStruct((64, 128), F32), j...]
where the time goes in v2:
time: 58.8 us; the launch traced here: 58.7 us
  Pallas kernels  56.7 us (96%)
  between operations  1.93 us (3%)
    pallas_call x1, Pallas kernels, per_device(): pl.pallas_call(kernel, out_shape=tuple((pltpu.VMEM(block, F32) for block...  56.1 us

profile of v2, /device:TPU:1, one launch (start us, length us, event | category | flops | bytes accessed | tf_op | source)
XLA Modules:
  0.0 58.7 jit_solution(10585660194678918819)
XLA Ops:
  1.9 56.1 %gauss_newton.1 = (f32[64,128]{1,0:T(8,128)S(1)}, f32[64,128]{1,0:T(8,128)S(1)}, f32[8,64]{1,0:T(8,128)S(1)}) custom-call(s32[3,4]{1,0:T(4,128)} %coords_hbm.1, s32[1]{0:T(128)S(6)} %copy.10.counts_hbm, f32[1]{0:T(128)} %bitcast.3.damp_hbm, f32[64,128]{1,0:T(8,128)} %fa_hbm.1, f32[64,128]{1,0:T(8,128)} %fb_hbm.1, f32[8,64]{1,0:T(8,128)} %bitcast.4, ...), custom_call_target="tpu_custom_call" | custom-call | tf_op jit(solution)/shard_map/gauss_newton/pallas_call | solution.py:440
  58.0 0.6 %put.1 = (f32[64,128]{1,0:T(8,128)}, f32[64,128]{1,0:T(8,128)}, f32[8,64]{1,0:T(8,128)}) custom-call(f32[64,128]{1,0:T(8,128)S(1)} %get-tuple-element.9.a, f32[64,128]{1,0:T(8,128)S(1)} %get-tuple-element.10.b, f32[8,64]{1,0:T(8,128)S(1)} %get-tuple-element.11.c), custom_call_target="tpu_custom_call" | custom-call | tf_op jit(solution)/shard_map/put/pallas_call | solution.py:471

commit v3 on v2

v3 whole, which is shorter than its diff:
```python
import jax
import jax.numpy as jnp
from jax import lax
from jax.experimental import pallas as pl
from jax.experimental.pallas import tpu as pltpu
from jax.sharding import PartitionSpec as P

G = 16
T = 4
RS = 4
F32 = jnp.float32
BF16 = jnp.bfloat16

COL_PEERS = [(dz, dc) for dz in (4, 3, 5, 2, 6, 1, 7) for dc in (0, 1)] + [(0, 1)]
ROW_PEERS = sorted(
    [(dy, dx) for dy in range(4) for dx in range(4) if (dy, dx) != (0, 0)],
    key=lambda d: -(min(d[0], 4 - d[0]) + min(d[1], 4 - d[1])),
)

PARTS = 1
SLOTS = [tuple(range(T // PARTS * i, T // PARTS * (i + 1))) for i in range(PARTS)]


def slot_boxes(name):
    return [(name + str(i), 0, 16 // PARTS) for i in range(PARTS)]


EXCHANGES = (
    ("a_slices", 0, 8), ("c_own", 1, 4), ("b_slices", 1, 8),
    *slot_boxes("a_slots"), ("b_slots", 1, 16), ("c_slots", 0, 4),
    *slot_boxes("ga_in"), ("gc_in", 1, 4), ("gb_in", 1, 16),
    *slot_boxes("ga_out"), ("gb_out", 1, 16), ("gc_out", 0, 4),
    *slot_boxes("wa_in"), ("wc_in", 1, 4), ("wb_in", 1, 16),
    *slot_boxes("wa_out"), ("wb_out", 1, 16), ("wc_out", 0, 4),
    ("a_put", 0, 8), ("b_put", 1, 8), ("c_put", 0, 8),
    ("sum_col", 0, 1), ("sum_row", 1, 1),
)
INDEX = {name: i for i, (name, _, _) in enumerate(EXCHANGES)}


def mm(a, b, rhs_dim=0):
    return lax.dot_general(a, b, (((1,), (rhs_dim,)), ((), ())), preferred_element_type=F32)


def split(x, count, axis):
    parts = []
    for _ in range(count):
        part = x.astype(BF16)
        parts.append(part)
        x = x - part.astype(F32)
    return parts if axis is None else jnp.concatenate(parts, axis=axis)


def left_of(x, axis=1):
    high, low = split(x, 2, None)
    return jnp.concatenate([high, high, low], axis=axis)


def right_of(x, axis):
    high, low = split(x, 2, None)
    return jnp.concatenate([high, low, high], axis=axis)


def iota(shape, dim):
    return lax.broadcasted_iota(jnp.int32, shape, dim)


def kernel(coords_hbm, counts_hbm, damp_hbm, fa_hbm, fb_hbm, fc_hbm, data_hbm, *refs):
    out_a, out_b, out_c = refs[:3]
    refs = refs[3:]
    n = len(EXCHANGES)
    outbox, inbox = refs[:n], refs[n:2 * n]
    (
        coords, counts, damp, fa, fb, fc, data,
        va, vb, ga, gb, ta, tb, da, db, jg,
        at3, tb3, tac3, bc3, left, xc,
        wa, wb, wat, wbt, same_a, same_b, mix, load_sem, send_sem, recv_sem,
    ) = refs[2 * n:]
    p = lax.axis_index("row")
    q = lax.axis_index("col")
    z, core = q // 2, q % 2
    col_of = [((z + dz) % 8) * 2 + (core + dc) % 2 for dz, dc in COL_PEERS]
    y, x = p // 4, p % 4
    row_of = [((y + dy) % 4) * 4 + (x + dx) % 4 for dy, dx in ROW_PEERS]

    barrier = pltpu.get_barrier_semaphore()
    for peer in col_of:
        pl.semaphore_signal(barrier, inc=1, device_id={"col": peer})
    for peer in row_of:
        pl.semaphore_signal(barrier, inc=1, device_id={"row": peer})

    loads = [
        pltpu.make_async_copy(src, dst, load_sem.at[i])
        for i, (src, dst) in enumerate((
            (coords_hbm, coords), (counts_hbm, counts), (damp_hbm, damp),
            (fa_hbm, fa), (fb_hbm, fb), (fc_hbm, fc), (data_hbm, data),
        ))
    ]
    for load in loads:
        load.start()

    def box(name):
        return outbox[INDEX[name]], inbox[INDEX[name]]

    def send(name):
        i = INDEX[name]
        me, peers, axis = ((q, col_of, "col"), (p, row_of, "row"))[EXCHANGES[i][1]]
        src, dst = outbox[i], inbox[i]
        for peer in peers:
            pltpu.make_async_remote_copy(
                src_ref=src.at[peer],
                dst_ref=dst.at[me],
                send_sem=send_sem.at[i],
                recv_sem=recv_sem.at[i],
                device_id={axis: peer},
            ).start()
        dst[me] = src[me]

    def wait(sem, ref):
        some = ref.at[pl.ds(0, G - 1)]
        pltpu.make_async_copy(some, some, sem).wait()

    def arrived(name):
        i = INDEX[name]
        wait(recv_sem.at[i], inbox[i])
        return inbox[i]

    lane = iota((1, 128), 1)
    zero_row = jnp.zeros((1, 128), F32)

    def positions(coord_row, member, groups):
        wide = 16 // len(groups)
        lanes = iota((1, 256), 1)
        val = jnp.zeros((1, 256), F32)
        for g, slots in enumerate(groups):
            for i, t in enumerate(slots):
                here = lanes - (256 // len(groups) * g + member * wide + RS * i)
                at = (here >= 0) & (here < RS)
                val = jnp.where(at, (coords[coord_row, t] * RS + here).astype(F32), val)
        return val[:, 0:128], val[:, 128:256]

    def depth_index(member):
        here = lane - member * 8
        val = zero_row
        for t in range(T):
            at = (here == t) | (here == t + T)
            val = jnp.where(at, coords[2, t].astype(F32), val)
        return val

    loads[0].wait()
    first, second = positions(0, q, SLOTS)
    info_col = jnp.concatenate([first, second, depth_index(q), zero_row], axis=0)
    first, second = positions(1, p, [range(T)])
    info_row = jnp.concatenate([first, second, depth_index(p), zero_row], axis=0)
    for load in loads[3:6]:
        load.wait()
    own = jnp.concatenate([fc[0:4], fc[4:8]], axis=1)
    a_slices, c_own, b_slices = box("a_slices")[0], box("c_own")[0], box("b_slices")[0]
    for j in range(G):
        a_slices[j, 0:4] = fa[4 * j:4 * j + 4]
        a_slices[j, 4:8] = info_col
        c_own[j] = own
        b_slices[j, 0:4] = fb[4 * j:4 * j + 4]
        b_slices[j, 4:8] = info_row

    pl.semaphore_wait(barrier, 2 * (G - 1))
    send("a_slices")
    send("b_slices")
    send("c_own")

    def across_of(info):
        return jnp.concatenate([info[4:5], info[5:6]], axis=1).astype(jnp.int32)

    lane64 = iota((128, 192), 1) % 64

    def back_matrix(info, dst):
        turned = jnp.transpose(info).astype(jnp.int32)
        for half in range(2):
            here = turned[:, 4 + half:5 + half]
            dst[128 * half:128 * half + 128] = (lane64 == here).astype(BF16)
        return turned

    def names_of(name):
        return [name + str(i) for i in range(PARTS)]

    def serve_blocks(w, v, names):
        parts = split(v, 3, 0)
        size = 256 // len(names)
        for i, name in enumerate(names):
            total = mm(w[size * i:size * i + size], parts)
            box(name)[0][...] = total.reshape(G, -1, 128)
            send(name)

    def serve(same, rows, names):
        high, mid, low = split(rows, 3, None)
        most = jnp.concatenate([high, mid], axis=1)
        size = 256 // len(names)
        for i, name in enumerate(names):
            w = same[size * i:size * i + size]
            both = mm(w, most)
            total = both[:, 0:128] + (both[:, 128:256] + mm(w, low))
            box(name)[0][...] = total.reshape(G, -1, 128)
            send(name)

    def rows_of(names):
        boxes = [arrived(name) for name in names]
        return jnp.concatenate([ref[...].reshape(-1, 128) for ref in boxes], axis=0)

    def stacked(src):
        for j in range(G):
            xc[4 * j:4 * j + 4] = src[j]
        return xc[...]

    src = arrived("b_slices")
    info_row = jnp.sum(src[...], axis=0)
    turned_row = back_matrix(info_row, wbt)
    for j in range(G):
        vb[4 * j:4 * j + 4] = src[j, 0:4]
    serve_blocks(wbt, vb[...], ["b_slots"])
    columns_here = split(stacked(arrived("c_own")), 3, 0)
    src = arrived("a_slices")
    info_col = jnp.sum(src[...], axis=0)
    turned_col = back_matrix(info_col, wat)
    k_there = turned_col[:, 6:7]
    down, lane64 = iota((128, 192), 0), iota((128, 192), 1) % 64
    column = (lane64 // 4) * 128 + q * 8 + lane64 % 4
    wanted = jnp.where(down % 8 < T, k_there, -1)
    pick = jnp.concatenate(
        [(wanted == column).astype(BF16), (wanted == column + 4).astype(BF16)], axis=0
    )
    both = mm(pick, columns_here)
    c_out = box("c_slots")[0]
    c_out[...] = (pltpu.roll(both[:128], 64, 1) + both[128:]).reshape(G, 8, 128)[:, 0:4]
    send("c_slots")
    for j in range(G):
        va[4 * j:4 * j + 4] = src[j, 0:4]
    serve_blocks(wat, va[...], names_of("a_slots"))

    for info, turn, w, same in (
        (info_col, turned_col, wa, same_a), (info_row, turned_row, wb, same_b)
    ):
        across = across_of(info)
        w[...] = (iota((64, 256), 0) == across).astype(BF16)
        for half in range(2):
            here = turn[:, 4 + half:5 + half]
            same[128 * half:128 * half + 128] = (
                jnp.broadcast_to(across, (128, 256)) == here
            ).astype(BF16)

    spread = (iota((128, 192), 0) == (lane64 // 4) * 8 + lane64 % 4).astype(BF16)
    k_tiles = jnp.broadcast_to(info_row[6:7], (8, 128))
    k_lane = mm(split(k_tiles, 3, 1), jnp.concatenate([spread, spread, spread], axis=0))
    k_lane = jnp.broadcast_to(k_lane[0:1].astype(jnp.int32), (128, 192))
    mix[0:128] = (k_lane == p * 128 + down).astype(BF16)
    mix[128:256] = (k_lane == wanted).astype(BF16)

    def unpack(src, dst, slots):
        for i, t in enumerate(slots):
            for j in range(G):
                dst[t, 4 * j:4 * j + 4] = src[j, 4 * i:4 * i + 4]

    def pack(i, value, dst):
        for j in range(G):
            dst[j, 4 * i:4 * i + 4] = value[4 * j:4 * j + 4]

    def turned_of(rows):
        return jnp.transpose(jnp.concatenate([rows, jnp.zeros((4, 128), F32)], axis=0))

    def columns(turned):
        return [jnp.broadcast_to(turned[64:128, t:t + 1], (64, 128)) for t in range(T)]

    src = arrived("b_slots")
    unpack(src, tb, range(T))
    for t in range(T):
        tb3[t] = left_of(tb[t])
    src = arrived("c_slots")
    depth = columns(turned_of(jnp.sum(src[...], axis=0)))
    for t in range(T):
        bc3[t] = right_of(tb[t] * depth[t], 0)
    for load in (loads[1], loads[2], loads[6]):
        load.wait()

    def norm(value):
        return jnp.sum(value, axis=(0, 1), keepdims=True)

    def live(t):
        return (t < counts[0]).astype(F32)

    def gradients(values_of, name, scalars_of):
        gc_out, gb_out = box(name + "c_in")[0], box(name + "b_in")[0]
        cols = jnp.zeros((64, 128), F32)
        lanes = iota((64, 128), 1)
        for number, slots in enumerate(SLOTS):
            parts = [split(values, 2, None) for values in values_of(number, slots)]
            ga_name = name + "a_in" + str(number)
            for i, t in enumerate(slots):
                high, low = parts[i]
                raw = mm(tb3[t], jnp.concatenate([high, low, high], axis=1), 1)
                pack(i, raw * depth[t], box(ga_name)[0])
                col = jnp.sum(ta[t] * raw, axis=1, keepdims=True)
                cols = jnp.where(lanes == t, col, cols)
            send(ga_name)
            if slots[-1] == T - 1:
                tile = jnp.transpose(jnp.concatenate([cols, jnp.zeros((64, 128), F32)], axis=0))[:4]
                row4, lane4 = iota((4, 128), 0), iota((4, 128), 1)
                for i, scalar in enumerate(scalars_of()):
                    tile = jnp.where((row4 == i) & (lane4 >= 64), scalar, tile)
                for j in range(G):
                    gc_out[j] = tile
                send(name + "c_in")
            for i, t in enumerate(slots):
                high, low = parts[i]
                pack(t, mm(tac3[t], jnp.concatenate([high, low, high], axis=0)), gb_out)
        send(name + "b_in")
        return cols

    def data_left(number, slots):
        src = arrived("a_slots" + str(number))
        unpack(src, ta, slots)
        values = []
        for t in slots:
            at3[t] = left_of(jnp.transpose(ta[t]))
            tac3[t] = left_of(ta[t] * depth[t])
            values.append((data[t].astype(F32) - mm(at3[t], bc3[t])) * live(t))
        return values

    cols_g = gradients(data_left, "g", lambda: ())
    for t in range(T):
        for part in range(3):
            left[t, :, 128 * part + 64:128 * part + 128] = at3[t, :, 64 * part:64 * part + 64]

    def fold(w, rows, v):
        high, mid, low = split(rows, 3, None)
        most = mm(w[...], jnp.concatenate([high, mid], axis=1))
        v[...] = most[:, 0:128] + (most[:, 128:256] + mm(w[...], low))

    def blend(src):
        both = mm(mix[...], split(stacked(src), 3, 0))
        return jnp.where(iota((128, 128), 1) < 64, both[:128], pltpu.roll(both[128:], 64, 1))

    lane_col = iota((1, 1, 128), 2)

    def send_sums(name, u, base, scalars):
        own = pltpu.roll(u, 64, 1).reshape(G, 8, 128)
        u = u.reshape(G, 8, 128)
        c_put[:, base:base + 4] = jnp.where(lane_col < 64, u[:, 0:4], own[:, 4:8])
        now = u[:, 0:4]
        for i, scalar in enumerate(scalars):
            at = (iota((1, 4, 128), 1) == i) & (iota((1, 4, 128), 2) < 64)
            now = jnp.where(at, jnp.broadcast_to(scalar.reshape(1, 1, 1), (1, 4, 128)), now)
        box(name + "c_out")[0][...] = now
        send(name + "c_out")

    c_put = box("c_put")[0]

    src = arrived("gc_in")
    send_sums("g", blend(src), 0, ())
    rows_b = rows_of(["gb_in"])
    serve(same_b, rows_b, ["gb_out"])
    rows_a = rows_of(names_of("ga_in"))
    serve(same_a, rows_a, names_of("ga_out"))
    fold(wb, rows_b, gb)
    fold(wa, rows_a, ga)
    g_part = norm(ga[...] * ga[...] + gb[...] * gb[...])

    def direction_bc(name):
        src = arrived(name + "b_out")
        unpack(src, db, range(T))
        src = arrived(name + "c_out")
        total = jnp.sum(src[...], axis=0)
        turned = turned_of(total)
        du = columns(turned)
        rights = []
        for t in range(T):
            high, low = split(db[t] * depth[t] + tb[t] * du[t], 2, None)
            rights.append(jnp.concatenate(
                [bc3[t, 0:64], high, bc3[t, 64:128], low, bc3[t, 0:64], high], axis=0
            ))
        return total, turned[64:128], rights

    def direction_a(name, rights, number, slots):
        src = arrived(name + "a_out" + str(number))
        unpack(src, da, slots)
        products = []
        for t in slots:
            high, low = split(jnp.transpose(da[t]), 2, None)
            left[t, :, 0:64] = high
            left[t, :, 128:192] = high
            left[t, :, 256:320] = low
            products.append(mm(left[t], rights[t]) * live(t))
        return products

    _, dirs_g, rights = direction_bc("g")
    g_part = g_part + norm(cols_g[:, 0:8] * dirs_g)

    def second_values(number, slots):
        products = direction_a("g", rights, number, slots)
        for t, product in zip(slots, products):
            jg[t] = product
        return products

    def first_scalars():
        squares = jnp.zeros((128, 128), F32)
        for t in range(T):
            squares = squares + jg[t] * jg[t]
        return g_part, norm(squares)

    cols_w = gradients(second_values, "w", first_scalars)

    src = arrived("wc_in")
    group = jnp.sum(src[...], axis=0)
    send_sums("w", blend(src), 4, (group[0:1, 127:128], group[1:2, 127:128]))
    rows_b = rows_of(["wb_in"])
    serve(same_b, rows_b, ["wb_out"])
    rows_a = rows_of(names_of("wa_in"))
    serve(same_a, rows_a, names_of("wa_out"))
    fold(wb, rows_b, vb)
    fold(wa, rows_a, va)
    total_w, dirs_w, rights = direction_bc("w")
    lam = damp[0]
    g_norm = total_w[0:1, 0:1]
    j_norm = total_w[1:2, 0:1]
    alpha0 = g_norm / (j_norm + lam * g_norm)

    def residual_of(g, w):
        return g - alpha0 * (w + lam * g)

    r_a = residual_of(ga[...], va[...])
    r_b = residual_of(gb[...], vb[...])
    r_cols = residual_of(cols_g[:, 0:8], cols_w[:, 0:8])
    rr_part = norm(r_a * r_a + r_b * r_b) + norm(r_cols * residual_of(dirs_g, dirs_w))
    rg_part = norm(r_a * ga[...] + r_b * gb[...]) + norm(r_cols * dirs_g)
    square = jnp.zeros((128, 128), F32)
    cross = jnp.zeros((128, 128), F32)
    for number, slots in enumerate(SLOTS):
        for t, product in zip(slots, direction_a("w", rights, number, slots)):
            jr = residual_of(jg[t], product)
            square = square + jr * jr
            cross = cross + jr * jg[t]

    parts = (rr_part, rg_part, norm(square), norm(cross))
    row = zero_row
    for i, part in enumerate(parts):
        row = jnp.where(lane // 32 == i, part, row)
    out = box("sum_col")[0]
    for j in range(G):
        out[j] = row
    send("sum_col")
    a_put, b_put = box("a_put")[0], box("b_put")[0]
    for j in range(G):
        a_put[j, 0:4] = ga[4 * j:4 * j + 4]
        a_put[j, 4:8] = va[4 * j:4 * j + 4]
        b_put[j, 0:4] = gb[4 * j:4 * j + 4]
        b_put[j, 4:8] = vb[4 * j:4 * j + 4]
    send("a_put")
    send("b_put")
    send("c_put")

    src = arrived("sum_col")
    row = jnp.sum(src[...], axis=0)
    out = box("sum_row")[0]
    for j in range(G):
        out[j] = row
    send("sum_row")
    src_a = arrived("a_put")
    src_b = arrived("b_put")
    own = jnp.sum(arrived("c_put")[...], axis=0)
    own_g = jnp.concatenate([own[0:4, 0:64], own[0:4, 64:128]], axis=0)
    own_w = jnp.concatenate([own[4:8, 0:64], own[4:8, 64:128]], axis=0)
    for j in range(G):
        ga[4 * j:4 * j + 4] = src_a[j, 0:4]
        va[4 * j:4 * j + 4] = src_a[j, 4:8]
        gb[4 * j:4 * j + 4] = src_b[j, 0:4]
        vb[4 * j:4 * j + 4] = src_b[j, 4:8]
    blocks = ((ga[...], va[...], out_a), (gb[...], vb[...], out_b), (own_g, own_w, out_c))
    bases = [(alpha0 * g, residual_of(g, w), g, out) for g, w, out in blocks]
    src = arrived("sum_row")
    row = jnp.sum(src[...], axis=0)
    r_norm, r_g, jr_norm, jr_jg = [row[:, 32 * i:32 * i + 1] for i in range(4)]
    beta = r_norm / g_norm
    curve = (
        jr_norm + lam * r_norm
        + 2.0 * beta * (jr_jg + lam * r_g)
        + beta * beta * (j_norm + lam * g_norm)
    )
    alpha1 = r_norm / curve

    for base, r, g, out in bases:
        out[...] = base + alpha1 * (r + beta * g)
    for i in range(n):
        wait(send_sem.at[i], outbox[i])


def put(a, b, c, x, y, z):
    x[...] = a[...]
    y[...] = b[...]
    z[...] = c[...]


def per_device(
    tile_data, tile_coords, tile_counts, factor_rows, factor_cols, factor_depth, damping
):
    vmem = pl.BlockSpec(memory_space=pltpu.VMEM)
    boxes = [pltpu.VMEM((G, rows, 128), F32) for _, _, rows in EXCHANGES]
    blocks = ((64, 128), (64, 128), (8, 64))
    steps = pl.pallas_call(
        kernel,
        out_shape=tuple(pltpu.VMEM(block, F32) for block in blocks),
        in_specs=[pl.BlockSpec(memory_space=pltpu.HBM)] * 7,
        out_specs=(vmem, vmem, vmem),
        scratch_shapes=[
            *boxes, *boxes,
            pltpu.SMEM((3, T), jnp.int32), pltpu.SMEM((1,), jnp.int32), pltpu.SMEM((1,), F32),
            pltpu.VMEM((64, 128), F32), pltpu.VMEM((64, 128), F32), pltpu.VMEM((8, 64), F32),
            pltpu.VMEM((T, 128, 128), BF16),
            *[pltpu.VMEM((64, 128), F32)] * 4,
            *[pltpu.VMEM((T, 64, 128), F32)] * 4,
            pltpu.VMEM((T, 128, 128), F32),
            pltpu.VMEM((T, 128, 192), BF16),
            pltpu.VMEM((T, 64, 384), BF16), pltpu.VMEM((T, 64, 384), BF16),
            pltpu.VMEM((T, 192, 128), BF16),
            pltpu.VMEM((T, 128, 384), BF16),
            pltpu.VMEM((64, 128), F32),
            pltpu.VMEM((64, 256), BF16), pltpu.VMEM((64, 256), BF16),
            pltpu.VMEM((256, 192), BF16), pltpu.VMEM((256, 192), BF16),
            pltpu.VMEM((256, 256), BF16), pltpu.VMEM((256, 256), BF16),
            pltpu.VMEM((256, 192), BF16),
            pltpu.SemaphoreType.DMA((7,)),
            pltpu.SemaphoreType.DMA((len(EXCHANGES),)),
            pltpu.SemaphoreType.DMA((len(EXCHANGES),)),
        ],
        compiler_params=pltpu.CompilerParams(collective_id=0, has_side_effects=True),
        name="gauss_newton",
    )(
        tile_coords, tile_counts, damping.reshape(1),
        factor_rows, factor_cols, factor_depth.T, tile_data,
    )
    step_a, step_b, step_c = pl.pallas_call(
        put,
        out_shape=tuple(jax.ShapeDtypeStruct(block, F32) for block in blocks),
        in_specs=[vmem, vmem, vmem],
        out_specs=(vmem, vmem, vmem),
        name="put",
    )(*[pltpu.with_memory_space_constraint(step, pltpu.VMEM) for step in steps])
    return step_a, step_b, step_c.T


def solution(mesh):
    both = ("row", "col")
    flip = ("col", "row")
    return jax.shard_map(
        per_device,
        mesh=mesh,
        in_specs=(
            P(both, None, None), P(None, both), P(both),
            P(None, both), P(None, flip), P(None, both), P(),
        ),
        out_specs=(P(None, both), P(None, flip), P(None, both)),
        check_vma=False,
    )
```

time: 58.8 us -> 58.8 us (level)
  no operation moved by 1% of the time
where the time goes in v3:
time: 58.8 us; the launch traced here: 58.7 us
  Pallas kernels  56.8 us (97%)
  between operations  1.93 us (3%)
    pallas_call x1, Pallas kernels, per_device(): pl.pallas_call(kernel, out_shape=tuple((pltpu.VMEM(block, F32) for block...  56.1 us

profile of v3, /device:TPU:1, one launch (start us, length us, event | category | flops | bytes accessed | tf_op | source)
XLA Modules:
  0.0 58.7 jit_solution(13816751675346826065)
XLA Ops:
  1.9 56.1 %gauss_newton.1 = (f32[64,128]{1,0:T(8,128)S(1)}, f32[64,128]{1,0:T(8,128)S(1)}, f32[8,64]{1,0:T(8,128)S(1)}) custom-call(s32[3,4]{1,0:T(4,128)} %coords_hbm.1, s32[1]{0:T(128)S(6)} %copy.10.counts_hbm, f32[1]{0:T(128)} %bitcast.3.damp_hbm, f32[64,128]{1,0:T(8,128)} %fa_hbm.1, f32[64,128]{1,0:T(8,128)} %fb_hbm.1, f32[8,64]{1,0:T(8,128)} %bitcast.4, ...), custom_call_target="tpu_custom_call" | custom-call | tf_op jit(solution)/shard_map/gauss_newton/pallas_call | solution.py:506
  58.1 0.6 %put.1 = (f32[64,128]{1,0:T(8,128)}, f32[64,128]{1,0:T(8,128)}, f32[8,64]{1,0:T(8,128)}) custom-call(f32[64,128]{1,0:T(8,128)S(1)} %get-tuple-element.9.a, f32[64,128]{1,0:T(8,128)S(1)} %get-tuple-element.10.b, f32[8,64]{1,0:T(8,128)S(1)} %get-tuple-element.11.c), custom_call_target="tpu_custom_call" | custom-call | tf_op jit(solution)/shard_map/put/pallas_call | solution.py:538

commit v4 on v3

--- a/solution.py
+++ b/solution.py
@@ -11,10 +11,17 @@
 F32 = jnp.float32
 BF16 = jnp.bfloat16
 
-COL_PEERS = [(dz, dc) for dz in (4, 3, 5, 2, 6, 1, 7) for dc in (0, 1)] + [(0, 1)]
+def ring(d, size):
+    return min(d, size - d)
+
+
+COL_PEERS = sorted(
+    [(dz, dc) for dz in range(8) for dc in range(2) if (dz, dc) != (0, 0)],
+    key=lambda d: (-(ring(d[0], 8) + d[1]) if d[0] else 0, -d[1], d[0]),
+)
 ROW_PEERS = sorted(
     [(dy, dx) for dy in range(4) for dx in range(4) if (dy, dx) != (0, 0)],
-    key=lambda d: -(min(d[0], 4 - d[0]) + min(d[1], 4 - d[1])),
+    key=lambda d: (-(ring(d[0], 4) + ring(d[1], 4)), -ring(d[0], 4)),
 )
 
 PARTS = 1
@@ -73,7 +80,7 @@
     (
         coords, counts, damp, fa, fb, fc, data,
         va, vb, ga, gb, ta, tb, da, db, jg,
-        at3, tb3, tac3, bc3, left, xc,
+        bct3, tb3, tac3, a3, left, datat, xc,
         wa, wb, wat, wbt, same_a, same_b, mix, load_sem, send_sem, recv_sem,
     ) = refs[2 * n:]
     p = lax.axis_index("row")
@@ -276,9 +283,11 @@
     src = arrived("c_slots")
     depth = columns(turned_of(jnp.sum(src[...], axis=0)))
     for t in range(T):
-        bc3[t] = right_of(tb[t] * depth[t], 0)
+        bct3[t] = left_of(jnp.transpose(tb[t] * depth[t]))
     for load in (loads[1], loads[2], loads[6]):
         load.wait()
+    for t in range(T):
+        datat[t] = jnp.transpose(data[t].astype(F32))
 
     def norm(value):
         return jnp.sum(value, axis=(0, 1), keepdims=True)
@@ -295,7 +304,7 @@
             ga_name = name + "a_in" + str(number)
             for i, t in enumerate(slots):
                 high, low = parts[i]
-                raw = mm(tb3[t], jnp.concatenate([high, low, high], axis=1), 1)
+                raw = mm(tb3[t], jnp.concatenate([high, low, high], axis=0))
                 pack(i, raw * depth[t], box(ga_name)[0])
                 col = jnp.sum(ta[t] * raw, axis=1, keepdims=True)
                 cols = jnp.where(lanes == t, col, cols)
@@ -310,7 +319,7 @@
                 send(name + "c_in")
             for i, t in enumerate(slots):
                 high, low = parts[i]
-                pack(t, mm(tac3[t], jnp.concatenate([high, low, high], axis=0)), gb_out)
+                pack(t, mm(tac3[t], jnp.concatenate([high, low, high], axis=1), 1), gb_out)
         send(name + "b_in")
         return cols
 
@@ -319,15 +328,15 @@
         unpack(src, ta, slots)
         values = []
         for t in slots:
-            at3[t] = left_of(jnp.transpose(ta[t]))
+            a3[t] = right_of(ta[t], 0)
             tac3[t] = left_of(ta[t] * depth[t])
-            values.append((data[t].astype(F32) - mm(at3[t], bc3[t])) * live(t))
+            values.append((datat[t] - mm(bct3[t], a3[t])) * live(t))
         return values
 
     cols_g = gradients(data_left, "g", lambda: ())
     for t in range(T):
         for part in range(3):
-            left[t, :, 128 * part + 64:128 * part + 128] = at3[t, :, 64 * part:64 * part + 64]
+            left[t, :, 128 * part:128 * part + 64] = bct3[t, :, 64 * part:64 * part + 64]
 
     def fold(w, rows, v):
         high, mid, low = split(rows, 3, None)
@@ -370,31 +379,28 @@
         total = jnp.sum(src[...], axis=0)
         turned = turned_of(total)
         du = columns(turned)
-        rights = []
         for t in range(T):
-            high, low = split(db[t] * depth[t] + tb[t] * du[t], 2, None)
-            rights.append(jnp.concatenate(
-                [bc3[t, 0:64], high, bc3[t, 64:128], low, bc3[t, 0:64], high], axis=0
-            ))
-        return total, turned[64:128], rights
-
-    def direction_a(name, rights, number, slots):
+            high, low = split(jnp.transpose(db[t] * depth[t] + tb[t] * du[t]), 2, None)
+            left[t, :, 64:128] = high
+            left[t, :, 192:256] = high
+            left[t, :, 320:384] = low
+        return total, turned[64:128]
+
+    def direction_a(name, number, slots):
         src = arrived(name + "a_out" + str(number))
         unpack(src, da, slots)
         products = []
         for t in slots:
-            high, low = split(jnp.transpose(da[t]), 2, None)
-            left[t, :, 0:64] = high
-            left[t, :, 128:192] = high
-            left[t, :, 256:320] = low
-            products.append(mm(left[t], rights[t]) * live(t))
+            high, low = split(da[t], 2, None)
+            right = [high, a3[t, 0:64], low, a3[t, 64:128], high, a3[t, 0:64]]
+            products.append(mm(left[t], jnp.concatenate(right, axis=0)) * live(t))
         return products
 
-    _, dirs_g, rights = direction_bc("g")
+    _, dirs_g = direction_bc("g")
     g_part = g_part + norm(cols_g[:, 0:8] * dirs_g)
 
     def second_values(number, slots):
-        products = direction_a("g", rights, number, slots)
+        products = direction_a("g", number, slots)
         for t, product in zip(slots, products):
             jg[t] = product
         return products
@@ -416,7 +422,7 @@
     serve(same_a, rows_a, names_of("wa_out"))
     fold(wb, rows_b, vb)
     fold(wa, rows_a, va)
-    total_w, dirs_w, rights = direction_bc("w")
+    total_w, dirs_w = direction_bc("w")
     lam = damp[0]
     g_norm = total_w[0:1, 0:1]
     j_norm = total_w[1:2, 0:1]
@@ -433,7 +439,7 @@
     square = jnp.zeros((128, 128), F32)
     cross = jnp.zeros((128, 128), F32)
     for number, slots in enumerate(SLOTS):
-        for t, product in zip(slots, direction_a("w", rights, number, slots)):
+        for t, product in zip(slots, direction_a("w", number, slots)):
             jr = residual_of(jg[t], product)
             square = square + jr * jr
             cross = cross + jr * jg[t]
@@ -520,6 +526,7 @@
             pltpu.VMEM((T, 64, 384), BF16), pltpu.VMEM((T, 64, 384), BF16),
             pltpu.VMEM((T, 192, 128), BF16),
             pltpu.VMEM((T, 128, 384), BF16),
+            pltpu.VMEM((T, 128, 128), F32),
             pltpu.VMEM((64, 128), F32),
             pltpu.VMEM((64, 256), BF16), pltpu.VMEM((64, 256), BF16),
             pltpu.VMEM((256, 192), BF16), pltpu.VMEM((256, 192), BF16),

time: 58.8 us -> 57.3 us (0.974)
  Pallas kernels: 56.8 us -> 55.2 us
    pallas_call x1, Pallas kernels: 56.1 us -> 54.6 us  [per_device(): pl.pallas_call(kernel, out_shape=tuple((pltpu.VMEM(block, F32) for block...]
where the time goes in v4:
time: 57.3 us; the launch traced here: 57.2 us
  Pallas kernels  55.2 us (96%)
  between operations  1.93 us (3%)
    pallas_call x1, Pallas kernels, per_device(): pl.pallas_call(kernel, out_shape=tuple((pltpu.VMEM(block, F32) for block...  54.6 us

profile of v4, /device:TPU:1, one launch (start us, length us, event | category | flops | bytes accessed | tf_op | source)
XLA Modules:
  0.0 57.2 jit_solution(12402430959075049160)
XLA Ops:
  1.9 54.6 %gauss_newton.1 = (f32[64,128]{1,0:T(8,128)S(1)}, f32[64,128]{1,0:T(8,128)S(1)}, f32[8,64]{1,0:T(8,128)S(1)}) custom-call(s32[3,4]{1,0:T(4,128)} %coords_hbm.1, s32[1]{0:T(128)S(6)} %copy.10.counts_hbm, f32[1]{0:T(128)} %bitcast.3.damp_hbm, f32[64,128]{1,0:T(8,128)} %fa_hbm.1, f32[64,128]{1,0:T(8,128)} %fb_hbm.1, f32[8,64]{1,0:T(8,128)} %bitcast.4, ...), custom_call_target="tpu_custom_call" | custom-call | tf_op jit(solution)/shard_map/gauss_newton/pallas_call | solution.py:512
  56.5 0.6 %put.1 = (f32[64,128]{1,0:T(8,128)}, f32[64,128]{1,0:T(8,128)}, f32[8,64]{1,0:T(8,128)}) custom-call(f32[64,128]{1,0:T(8,128)S(1)} %get-tuple-element.9.a, f32[64,128]{1,0:T(8,128)S(1)} %get-tuple-element.10.b, f32[8,64]{1,0:T(8,128)S(1)} %get-tuple-element.11.c), custom_call_target="tpu_custom_call" | custom-call | tf_op jit(solution)/shard_map/put/pallas_call | solution.py:545

commit v5 on v4

--- a/solution.py
+++ b/solution.py
@@ -34,9 +34,9 @@
 
 EXCHANGES = (
     ("a_slices", 0, 8), ("c_own", 1, 4), ("b_slices", 1, 8),
-    *slot_boxes("a_slots"), ("b_slots", 1, 16), ("c_slots", 0, 4),
+    *slot_boxes("a_slots"), ("b_slots", 1, 16), ("c_slots", 0, 2),
     *slot_boxes("ga_in"), ("gc_in", 1, 4), ("gb_in", 1, 16),
-    *slot_boxes("ga_out"), ("gb_out", 1, 16), ("gc_out", 0, 4),
+    *slot_boxes("ga_out"), ("gb_out", 1, 16), ("gc_out", 0, 2),
     *slot_boxes("wa_in"), ("wc_in", 1, 4), ("wb_in", 1, 16),
     *slot_boxes("wa_out"), ("wb_out", 1, 16), ("wc_out", 0, 4),
     ("a_put", 0, 8), ("b_put", 1, 8), ("c_put", 0, 8),
@@ -213,6 +213,13 @@
         boxes = [arrived(name) for name in names]
         return jnp.concatenate([ref[...].reshape(-1, 128) for ref in boxes], axis=0)
 
+    def folded(u):
+        turned = pltpu.roll(u, 64, 1).reshape(G, 8, 128)
+        return jnp.where(iota((1, 1, 128), 2) < 64, turned[:, 0:2], u.reshape(G, 8, 128)[:, 2:4])
+
+    def unfolded(rows):
+        return jnp.concatenate([pltpu.roll(rows, 64, 1), rows], axis=0)
+
     def stacked(src):
         for j in range(G):
             xc[4 * j:4 * j + 4] = src[j]
@@ -237,7 +244,7 @@
     )
     both = mm(pick, columns_here)
     c_out = box("c_slots")[0]
-    c_out[...] = (pltpu.roll(both[:128], 64, 1) + both[128:]).reshape(G, 8, 128)[:, 0:4]
+    c_out[...] = folded(pltpu.roll(both[:128], 64, 1) + both[128:])
     send("c_slots")
     for j in range(G):
         va[4 * j:4 * j + 4] = src[j, 0:4]
@@ -281,7 +288,7 @@
     for t in range(T):
         tb3[t] = left_of(tb[t])
     src = arrived("c_slots")
-    depth = columns(turned_of(jnp.sum(src[...], axis=0)))
+    depth = columns(turned_of(unfolded(jnp.sum(src[...], axis=0))))
     for t in range(T):
         bct3[t] = left_of(jnp.transpose(tb[t] * depth[t]))
     for load in (loads[1], loads[2], loads[6]):
@@ -351,9 +358,11 @@
 
     def send_sums(name, u, base, scalars):
         own = pltpu.roll(u, 64, 1).reshape(G, 8, 128)
+        now = folded(u)
         u = u.reshape(G, 8, 128)
         c_put[:, base:base + 4] = jnp.where(lane_col < 64, u[:, 0:4], own[:, 4:8])
-        now = u[:, 0:4]
+        if scalars:
+            now = u[:, 0:4]
         for i, scalar in enumerate(scalars):
             at = (iota((1, 4, 128), 1) == i) & (iota((1, 4, 128), 2) < 64)
             now = jnp.where(at, jnp.broadcast_to(scalar.reshape(1, 1, 1), (1, 4, 128)), now)
@@ -377,7 +386,7 @@
         unpack(src, db, range(T))
         src = arrived(name + "c_out")
         total = jnp.sum(src[...], axis=0)
-        turned = turned_of(total)
+        turned = turned_of(total if total.shape[0] == 4 else unfolded(total))
         du = columns(turned)
         for t in range(T):
             high, low = split(jnp.transpose(db[t] * depth[t] + tb[t] * du[t]), 2, None)

time: 57.3 us -> 57 us (level)
  no operation moved by 1% of the time
where the time goes in v5:
time: 57 us; the launch traced here: 56.9 us
  Pallas kernels  55 us (96%)
  between operations  1.93 us (3%)
    pallas_call x1, Pallas kernels, per_device(): pl.pallas_call(kernel, out_shape=tuple((pltpu.VMEM(block, F32) for block...  54.3 us

profile of v5, /device:TPU:1, one launch (start us, length us, event | category | flops | bytes accessed | tf_op | source)
XLA Modules:
  0.0 56.9 jit_solution(11392477404684294053)
XLA Ops:
  1.9 54.3 %gauss_newton.1 = (f32[64,128]{1,0:T(8,128)S(1)}, f32[64,128]{1,0:T(8,128)S(1)}, f32[8,64]{1,0:T(8,128)S(1)}) custom-call(s32[3,4]{1,0:T(4,128)} %coords_hbm.1, s32[1]{0:T(128)S(6)} %copy.10.counts_hbm, f32[1]{0:T(128)} %bitcast.3.damp_hbm, f32[64,128]{1,0:T(8,128)} %fa_hbm.1, f32[64,128]{1,0:T(8,128)} %fb_hbm.1, f32[8,64]{1,0:T(8,128)} %bitcast.4, ...), custom_call_target="tpu_custom_call" | custom-call | tf_op jit(solution)/shard_map/gauss_newton/pallas_call | solution.py:521
  56.2 0.6 %put.1 = (f32[64,128]{1,0:T(8,128)}, f32[64,128]{1,0:T(8,128)}, f32[8,64]{1,0:T(8,128)}) custom-call(f32[64,128]{1,0:T(8,128)S(1)} %get-tuple-element.9.a, f32[64,128]{1,0:T(8,128)S(1)} %get-tuple-element.10.b, f32[8,64]{1,0:T(8,128)S(1)} %get-tuple-element.11.c), custom_call_target="tpu_custom_call" | custom-call | tf_op jit(solution)/shard_map/put/pallas_call | solution.py:554

commit v6 on v5

--- a/solution.py
+++ b/solution.py
@@ -43,6 +43,14 @@
     ("sum_col", 0, 1), ("sum_row", 1, 1),
 )
 INDEX = {name: i for i, (name, _, _) in enumerate(EXCHANGES)}
+
+AFTER = {
+    "wa_in0": "ga_in0", "wb_in": "gb_in", "wc_in": "gc_in", "wa_out0": "ga_out0", "wb_out": "gb_out",
+    "a_put": "a_slices", "b_put": "b_slices", "c_put": "c_slots",
+    "sum_col": "a_slots0", "sum_row": "c_own",
+}
+FIRST = [name for name, _, _ in EXCHANGES if name not in AFTER]
+SEM = {name: FIRST.index(AFTER.get(name, name)) for name, _, _ in EXCHANGES}
 
 
 def mm(a, b, rhs_dim=0):
@@ -117,8 +125,8 @@
             pltpu.make_async_remote_copy(
                 src_ref=src.at[peer],
                 dst_ref=dst.at[me],
-                send_sem=send_sem.at[i],
-                recv_sem=recv_sem.at[i],
+                send_sem=send_sem.at[SEM[name]],
+                recv_sem=recv_sem.at[SEM[name]],
                 device_id={axis: peer},
             ).start()
         dst[me] = src[me]
@@ -129,8 +137,15 @@
 
     def arrived(name):
         i = INDEX[name]
-        wait(recv_sem.at[i], inbox[i])
+        wait(recv_sem.at[SEM[name]], inbox[i])
         return inbox[i]
+
+    left_over = [name for name, _, _ in EXCHANGES]
+
+    def settle(*names):
+        for name in names:
+            wait(send_sem.at[SEM[name]], outbox[INDEX[name]])
+            left_over.remove(name)
 
     lane = iota((1, 128), 1)
     zero_row = jnp.zeros((1, 128), F32)
@@ -379,6 +394,7 @@
     serve(same_a, rows_a, names_of("ga_out"))
     fold(wb, rows_b, gb)
     fold(wa, rows_a, ga)
+    settle("ga_in0", "gb_in", "gc_in", "a_slices", "b_slices", "c_own", "c_slots", "a_slots0")
     g_part = norm(ga[...] * ga[...] + gb[...] * gb[...])
 
     def direction_bc(name):
@@ -421,6 +437,7 @@
         return g_part, norm(squares)
 
     cols_w = gradients(second_values, "w", first_scalars)
+    settle("ga_out0", "gb_out")
 
     src = arrived("wc_in")
     group = jnp.sum(src[...], axis=0)
@@ -502,8 +519,7 @@
 
     for base, r, g, out in bases:
         out[...] = base + alpha1 * (r + beta * g)
-    for i in range(n):
-        wait(send_sem.at[i], outbox[i])
+    settle(*list(left_over))
 
 
 def put(a, b, c, x, y, z):
@@ -542,8 +558,8 @@
             pltpu.VMEM((256, 256), BF16), pltpu.VMEM((256, 256), BF16),
             pltpu.VMEM((256, 192), BF16),
             pltpu.SemaphoreType.DMA((7,)),
-            pltpu.SemaphoreType.DMA((len(EXCHANGES),)),
-            pltpu.SemaphoreType.DMA((len(EXCHANGES),)),
+            pltpu.SemaphoreType.DMA((len(FIRST),)),
+            pltpu.SemaphoreType.DMA((len(FIRST),)),
         ],
         compiler_params=pltpu.CompilerParams(collective_id=0, has_side_effects=True),
         name="gauss_newton",

time: 57 us -> 56.8 us (level)
  no operation moved by 1% of the time
where the time goes in v6:
time: 56.8 us; the launch traced here: 56.7 us
  Pallas kernels  54.8 us (96%)
  between operations  1.93 us (3%)
    pallas_call x1, Pallas kernels, per_device(): pl.pallas_call(kernel, out_shape=tuple((pltpu.VMEM(block, F32) for block...  54.1 us

profile of v6, /device:TPU:1, one launch (start us, length us, event | category | flops | bytes accessed | tf_op | source)
XLA Modules:
  0.0 56.7 jit_solution(9557240356688435384)
XLA Ops:
  1.9 54.1 %gauss_newton.1 = (f32[64,128]{1,0:T(8,128)S(1)}, f32[64,128]{1,0:T(8,128)S(1)}, f32[8,64]{1,0:T(8,128)S(1)}) custom-call(s32[3,4]{1,0:T(4,128)} %coords_hbm.1, s32[1]{0:T(128)S(6)} %copy.10.counts_hbm, f32[1]{0:T(128)} %bitcast.3.damp_hbm, f32[64,128]{1,0:T(8,128)} %fa_hbm.1, f32[64,128]{1,0:T(8,128)} %fb_hbm.1, f32[8,64]{1,0:T(8,128)} %bitcast.4, ...), custom_call_target="tpu_custom_call" | custom-call | tf_op jit(solution)/shard_map/gauss_newton/pallas_call | solution.py:537
  56.1 0.6 %put.1 = (f32[64,128]{1,0:T(8,128)}, f32[64,128]{1,0:T(8,128)}, f32[8,64]{1,0:T(8,128)}) custom-call(f32[64,128]{1,0:T(8,128)S(1)} %get-tuple-element.9.a, f32[64,128]{1,0:T(8,128)S(1)} %get-tuple-element.10.b, f32[8,64]{1,0:T(8,128)S(1)} %get-tuple-element.11.c), custom_call_target="tpu_custom_call" | custom-call | tf_op jit(solution)/shard_map/put/pallas_call | solution.py:570
